TPU v7x, 32 devices: a whole 2x2x4 slice. The times are simulated.
32 devices in a mesh: model: 4 (over z), data: 8 (over y, x, core).
Axes of the slice: x: 2, y: 2, z: 4, core: 2. Of those that a mesh axis runs over, the one named last changes fastest.
Arguments:
- emb_param: float32 [16384, 1024], P('model', 'data')
- head_param: float32 [1024, 16384], P('data', 'model')
- emb_grad: float32 [8, 16384, 1024], P('data', 'model')
- head_grad: float32 [8, 1024, 16384], P('data', None, 'model')
- emb_row: float32 [16384], P('model')
- emb_col: float32 [1024], P('data')
- head_row: float32 [16384], P('model')
- head_col: float32 [1024], P('data')
Outputs:
- output 1: float32 [16384, 1024], P('model', 'data')
- output 2: float32 [1024, 16384], P('data', 'model')
- output 3: float32 [16384], P('model')
- output 4: float32 [1024], P('data')
- output 5: float32 [16384], P('model')
- output 6: float32 [1024], P('data')
- output 7: bfloat16 [16384, 1024], P('model', 'data')
- output 8: bfloat16 [1024, 16384], P('data', 'model')
All inputs are finite; a program needn't handle non-finite values.
Results may differ from a plain program's by a relative error of at most 0.001.
Values sent between devices are 32-bit elements.
A program may use at most 1 GiB of HBM per device.

v0:
```python
import jax
import jax.numpy as jnp
from jax import lax
from jax.sharding import PartitionSpec as P

TRAIN_STEP = 10
DECAY_EXP = 0.8
EPS_ONE = 1e-30
CLIP_LIMIT = 1.0
SCALE_FLOOR = 1e-3
LEARN_RATE = float(TRAIN_STEP) ** -0.5
BETA_TWO = 1.0 - float(TRAIN_STEP) ** -DECAY_EXP


def apply_step(param, grad_sum, row_old, col_old, row_sq, col_sq, vocab_axis, vocab, embed):
    embed_axis = 1 - vocab_axis
    row_new = BETA_TWO * row_old + (1.0 - BETA_TWO) * (row_sq / embed)
    col_new = BETA_TWO * col_old + (1.0 - BETA_TWO) * (col_sq / vocab)
    row_mean = lax.psum(jnp.sum(row_new), "model") / vocab
    row_factor = jnp.expand_dims(lax.rsqrt(row_new), embed_axis)
    col_factor = jnp.expand_dims(lax.rsqrt(col_new) * jnp.sqrt(row_mean), vocab_axis)
    update = grad_sum * row_factor * col_factor
    update_rms = jnp.sqrt(lax.psum(jnp.sum(update * update), ("model", "data")) / (vocab * embed))
    param_rms = jnp.sqrt(lax.psum(jnp.sum(param * param), ("model", "data")) / (vocab * embed))
    step_size = LEARN_RATE * jnp.maximum(SCALE_FLOOR, param_rms) / jnp.maximum(1.0, update_rms / CLIP_LIMIT)
    return param - step_size * update, row_new, col_new


def block_update(param, grad_sum, row_old, col_old, vocab_axis, vocab, embed):
    embed_axis = 1 - vocab_axis
    grad_sq = grad_sum * grad_sum + EPS_ONE
    row_sq = lax.psum(jnp.sum(grad_sq, axis=embed_axis), "data")
    col_sq = lax.psum(jnp.sum(grad_sq, axis=vocab_axis), "model")
    return apply_step(param, grad_sum, row_old, col_old, row_sq, col_sq, vocab_axis, vocab, embed)


def solution(mesh):
    arg_specs = (P("model", "data"), P("data", "model"), P("data", "model", None), P("data", None, "model"),
                 P("model"), P("data"), P("model"), P("data"))
    result_specs = (P("model", "data"), P("data", "model"), P("model"), P("data"), P("model"), P("data"),
                    P("model", "data"), P("data", "model"))

    def update_tables(emb_param, head_param, emb_grad, head_grad, emb_row, emb_col, head_row, head_col):
        vocab = emb_param.shape[0]
        embed = emb_param.shape[1]

        def local_step(emb_block, head_block, emb_contrib, head_contrib, emb_rows, emb_cols, head_rows, head_cols):
            emb_sum = lax.psum_scatter(emb_contrib[0], "data", scatter_dimension=1, tiled=True)
            head_sum = lax.psum_scatter(head_contrib[0], "data", scatter_dimension=0, tiled=True)
            emb_new, emb_row_new, emb_col_new = block_update(emb_block, emb_sum, emb_rows, emb_cols, 0, vocab, embed)
            head_new, head_row_new, head_col_new = block_update(head_block, head_sum, head_rows, head_cols, 1, vocab, embed)
            return (emb_new, head_new, emb_row_new, emb_col_new, head_row_new, head_col_new,
                    emb_new.astype(jnp.bfloat16), head_new.astype(jnp.bfloat16))

        mapped = jax.shard_map(local_step, mesh=mesh, in_specs=arg_specs, out_specs=result_specs, check_vma=False)
        return mapped(emb_param, head_param, emb_grad, head_grad, emb_row, emb_col, head_row, head_col)

    return update_tables
```

profile of v0, /device:TPU:0, one launch (start us, length us, event | category | flops | bytes accessed | tf_op | source)
XLA Modules:
  0.0 346.2 jit_solution(9720281499739951767)
XLA Ops:
  7.2 0.0 reduce-scatter.5.cloned.1.call-start
  7.2 0.7 reduce-scatter.5.cloned.1.call-update
  7.9 0.0 reduce-scatter.3.cloned.1.call-start
  7.9 0.0 copy-start.2
  8.0 0.7 reduce-scatter.3.cloned.1.call-update
  8.6 0.9 copy-done.2
  9.5 0.0 copy-start.1
  9.5 1.1 multiply_reduce_fusion.1
  10.7 0.5 copy-done.1
  11.1 1.1 multiply_reduce_fusion.3
  12.3 0.0 copy-start.6
  12.3 0.0 copy-start.7
  12.3 0.0 copy-start.8
  12.3 0.0 copy-start.9
  12.3 117.4 %reduce-scatter.5.cloned.1.call-done = f32[128,4096]{1,0:T(8,128)} async-done(((f32[1024,4096]{1,0:T(8,128)}), f32[128,4096]{1,0:T(8,128)}) %reduce-scatter.5.cloned.1.call-update) | async-done | bytes 2097168 | tf_op jit(solution)/shard_map/reduce_scatter | solution.py:49
  129.7 2.0 fusion.3
  131.6 0.0 copy-start
  131.6 116.9 %reduce-scatter.3.cloned.1.call-done = f32[4096,128]{1,0:T(8,128)} async-done(((f32[4096,1024]{1,0:T(8,128)}), f32[4096,128]{1,0:T(8,128)}) %reduce-scatter.3.cloned.1.call-update) | async-done | bytes 2097168 | tf_op jit(solution)/shard_map/reduce_scatter | solution.py:48
  248.5 2.2 fusion.1
  250.7 22.8 %all-reduce.1 = (f32[4096]{0:T(1024)S(1)}, f32[4096]{0:T(1024)S(1)}) all-reduce(f32[4096]{0:T(1024)S(1)} %get-tuple-element.10, f32[4096]{0:T(1024)S(1)} %get-tuple-element.8), channel_id=1, replica_groups=mesh['model'=4,'data'=8] {'data'}, use_global_device_ids=true, to_apply=%region_4.0 | all-reduce | flops 8192 | bytes 65536 | tf_op jit(solution)/shard_map/psum | solution.py:32
  273.5 0.0 copy-done.6
  273.5 0.0 copy-done.7
  273.6 0.0 copy-start.4
  273.6 0.0 copy-start.5
  273.6 0.6 reduce_sum.93
  274.2 0.6 reduce_sum.98
  274.8 12.3 %all-reduce.2 = (f32[128]{0:T(128)S(1)}, f32[]{:T(128)}, f32[128]{0:T(128)S(1)}, f32[]{:T(128)}) all-reduce(f32[128]{0:T(128)S(1)} %get-tuple-element.11, f32[]{:T(128)} %reduce_sum.93, f32[128]{0:T(128)S(1)} %get-tuple-element.9, f32[]{:T(128)} %reduce_sum.98), channel_id=1, replica_groups=mesh['model'=4,'data'=8] {'model'}, use_global_device_ids=true, to_apply=%region_6.0 | all-reduce | flops 258 | bytes 2064 | tf_op jit(solution)/shard_map/psum | solution.py:33
  288.5 0.0 copy-done.8
  288.5 0.5 rsqrt_multiply_fusion.1
  289.0 0.0 copy-done.9
  289.0 0.5 rsqrt_multiply_fusion
  289.6 2.5 multiply_reduce_fusion.2
  292.1 0.0 copy-done
  292.1 1.3 multiply_reduce_fusion
  293.4 0.0 copy-done.4
  293.4 0.0 copy-done.5
  293.4 37.2 %all-reduce = (f32[]{:T(128)}, f32[]{:T(128)}, f32[]{:T(128)}, f32[]{:T(128)}) all-reduce(f32[]{:T(128)} %multiply_reduce_fusion.3, f32[]{:T(128)} %multiply_reduce_fusion.2, f32[]{:T(128)} %multiply_reduce_fusion.1, f32[]{:T(128)} %multiply_reduce_fusion), channel_id=1, replica_groups=mesh['model'=4,'data'=8] {'model','data'}, use_global_device_ids=true, to_apply=%region_1.0 | all-reduce | flops 4 | bytes 32 | tf_op jit(solution)/shard_map/psum | solution.py:24
  333.4 0.0 copy-start.3
  333.4 3.8 %fusion.5 = (bf16[4096,128]{1,0:T(8,128)(2,1)}, f32[4096,128]{1,0:T(8,128)}) fusion(f32[4096,128]{1,0:T(8,128)} %param.8, f32[128]{0:T(128)S(1)} %get-tuple-element.32, f32[4096,128]{1,0:T(8,128)} %reduce-scatter.3.cloned.1.call-done, f32[4096]{0:T(1024)S(1)} %get-tuple-element.34, f32[]{:T(128)S(6)} %div.33), kind=kLoop, calls=%fused_computation.21 | loop fusion | flops 2621440 | bytes 7356932 | tf_op jit(solution)/shard_map/convert_element_type | solution.py:53
  337.2 0.0 copy-done.3
  337.2 2.2 fusion.4
  (1 shorter events, 0.0 us)
Async XLA Ops:
  7.2 122.5 %reduce-scatter.5.cloned.1.call-start = ((), (), s32[]{:S(2)}) async-start(), calls=%async_computation.3 | async-start | bytes 18874368 | tf_op jit(solution)/shard_map/reduce_scatter | solution.py:49
  7.9 240.6 %reduce-scatter.3.cloned.1.call-start = ((), (), s32[]{:S(2)}) async-start(), calls=%async_computation.2 | async-start | bytes 18874368 | tf_op jit(solution)/shard_map/reduce_scatter | solution.py:48
  7.9 1.6 copy-start.2
  9.5 1.6 copy-start.1
  12.3 261.3 %copy-start.6 = (f32[4096]{0:T(1024)S(1)}, f32[4096]{0:T(1024)}, u32[]{:S(2)}) copy-start(f32[4096]{0:T(1024)} %param.14) | copy-start | bytes 49156
  12.3 261.3 %copy-start.7 = (f32[4096]{0:T(1024)S(1)}, f32[4096]{0:T(1024)}, u32[]{:S(2)}) copy-start(f32[4096]{0:T(1024)} %param.12) | copy-start | bytes 49156
  12.3 276.2 %copy-start.8 = (f32[128]{0:T(128)S(1)}, f32[128]{0:T(128)}, u32[]{:S(2)}) copy-start(f32[128]{0:T(128)} %param.13) | copy-start | bytes 1540
  12.3 276.8 %copy-start.9 = (f32[128]{0:T(128)S(1)}, f32[128]{0:T(128)}, u32[]{:S(2)}) copy-start(f32[128]{0:T(128)} %param.15) | copy-start | bytes 1540
  131.6 160.5 %copy-start = (f32[128,4096]{1,0:T(8,128)S(1)}, f32[128,4096]{1,0:T(8,128)}, u32[]{:S(2)}) copy-start(f32[128,4096]{1,0:T(8,128)} %reduce-scatter.5.cloned.1.call-done) | copy-start | bytes 6291460
  273.6 19.8 %copy-start.4 = (f32[4096]{0:T(1024)}, f32[4096]{0:T(1024)S(1)}, u32[]{:S(2)}) copy-start(f32[4096]{0:T(1024)S(1)} %get-tuple-element.27) | copy-start | bytes 49156
  273.6 19.8 %copy-start.5 = (f32[4096]{0:T(1024)}, f32[4096]{0:T(1024)S(1)}, u32[]{:S(2)}) copy-start(f32[4096]{0:T(1024)S(1)} %get-tuple-element.35) | copy-start | bytes 49156
  333.4 3.8 %copy-start.3 = (f32[128,4096]{1,0:T(8,128)S(1)}, f32[128,4096]{1,0:T(8,128)}, u32[]{:S(2)}) copy-start(f32[128,4096]{1,0:T(8,128)} %param.9) | copy-start | bytes 6291460
Sparse Core Ops, SparseCore 0:
  11.5 118.0 reduce-scatter.4
  133.2 115.2 reduce-scatter.2
where the time goes:
time: 347 us; the launch traced here: 346 us
  waiting for transfers between devices  236 us (68%)
  blocking collectives  72.3 us (21%)
  other arithmetic  18.5 us (5%)
  between operations  18.3 us (5%)
    reduce_scatter x1, waiting for transfers between devices, local_step(): lax.psum_scatter(head_contrib[0], 'data', scatter_dimension=0, tiled=True)  117 us
    reduce_scatter x1, waiting for transfers between devices, local_step(): lax.psum_scatter(emb_contrib[0], 'data', scatter_dimension=1, tiled=True)  117 us
    psum x1, blocking collectives, apply_step(): lax.psum(jnp.sum(param * param), ('model', 'data')) / (vocab * embed)  37.2 us
    psum x1, blocking collectives, block_update(): row_sq = lax.psum(jnp.sum(grad_sq, axis=embed_axis), 'data')  22.8 us
    psum x1, blocking collectives, block_update(): col_sq = lax.psum(jnp.sum(grad_sq, axis=vocab_axis), 'model')  12.3 us
  transfers between devices with their start and end apart: 2, of which 2 were waited for; matrix products, arithmetic and copies ran while one was open for 1% of the time, Pallas kernels for 0%

commit v1 on v0

--- a/solution.py
+++ b/solution.py
@@ -1,6 +1,10 @@
+import functools
+
 import jax
 import jax.numpy as jnp
 from jax import lax
+from jax.experimental import pallas as pl
+from jax.experimental.pallas import tpu as pltpu
 from jax.sharding import PartitionSpec as P
 
 TRAIN_STEP = 10
@@ -10,6 +14,170 @@
 SCALE_FLOOR = 1e-3
 LEARN_RATE = float(TRAIN_STEP) ** -0.5
 BETA_TWO = 1.0 - float(TRAIN_STEP) ** -DECAY_EXP
+
+MESH = pl.DeviceIdType.MESH
+CHUNK = 256
+AHEAD = 3
+LANES = 128
+
+
+class Table:
+    def __init__(self, grad, out, own, half, first_x, first_y, second_x, second_y, sems, rows):
+        self.grad, self.out, self.own, self.half = grad, out, own, half
+        self.first_x, self.first_y, self.second_x, self.second_y = first_x, first_y, second_x, second_y
+        self.ld, self.ra, self.rfx, self.rfy, self.rgx, self.rgy, self.snd, self.osem = sems
+        self.h = rows // 2
+
+
+def reduce_kernel(steps, emb_grad, head_grad, emb_out, head_out, *scratch):
+    emb_buf, head_buf = scratch[:6], scratch[6:12]
+    emb_sem, head_sem = scratch[12:20], scratch[20:28]
+    emb = Table(emb_grad, emb_out, *emb_buf, emb_sem, CHUNK)
+    head = Table(head_grad, head_out, *head_buf, head_sem, LANES)
+
+    z = lax.axis_index("model")
+    d = lax.axis_index("data")
+    c = lax.rem(d, 2)
+    x = lax.rem(d // 2, 2)
+    y = d // 4
+    partner = (z, d + 1 - 2 * c)
+    xnbr = (z, d + 2 - 4 * x)
+    ynbr = (z, d + 4 - 8 * y)
+
+    def emb_slice(k, yy, xx, core):
+        col = pl.multiple_of(((yy * 2 + xx) * 2 + core) * LANES, LANES)
+        return emb_grad.at[pl.ds(pl.multiple_of(k * CHUNK, CHUNK), CHUNK), pl.ds(col, LANES)]
+
+    def head_slice(k, core):
+        return head_grad.at[:, :, core, :, pl.ds(pl.multiple_of(k * CHUNK, CHUNK), CHUNK)]
+
+    def load(k, is_emb):
+        if is_emb:
+            for yy in range(2):
+                for xx in range(2):
+                    pltpu.make_async_copy(emb_slice(k, yy, xx, c), emb.own.at[k, yy, xx], emb.ld.at[k]).start()
+        else:
+            pltpu.make_async_copy(head_slice(k, c), head.own.at[k], head.ld.at[k]).start()
+
+    def exchange(k, is_emb):
+        if is_emb:
+            for yy in range(2):
+                for xx in range(2):
+                    pltpu.make_async_remote_copy(
+                        src_ref=emb_slice(k, yy, xx, 1 - c), dst_ref=emb.half.at[k, yy, xx],
+                        send_sem=emb.snd.at[0], recv_sem=emb.ra.at[k],
+                        device_id=partner, device_id_type=MESH).start()
+        else:
+            pltpu.make_async_remote_copy(
+                src_ref=head_slice(k, 1 - c), dst_ref=head.half.at[k],
+                send_sem=head.snd.at[0], recv_sem=head.ra.at[k],
+                device_id=partner, device_id_type=MESH).start()
+
+    def arrived(ref, sem):
+        pltpu.make_async_copy(ref, ref, sem).wait()
+
+    def first_hop(k, t):
+        arrived(t.own.at[k], t.ld.at[k])
+        arrived(t.half.at[k], t.ra.at[k])
+        h = t.h
+        for yy in range(2):
+            t.own[k, yy, 1 - x, :h] += t.half[k, yy, 1 - x, :h]
+        pltpu.make_async_remote_copy(
+            src_ref=t.own.at[k, :, 1 - x, pl.ds(0, h)], dst_ref=t.first_x.at[k],
+            send_sem=t.snd.at[1], recv_sem=t.rfx.at[k], device_id=xnbr, device_id_type=MESH).start()
+        for xx in range(2):
+            t.own[k, 1 - y, xx, h:] += t.half[k, 1 - y, xx, h:]
+        pltpu.make_async_remote_copy(
+            src_ref=t.own.at[k, 1 - y, :, pl.ds(h, h)], dst_ref=t.first_y.at[k],
+            send_sem=t.snd.at[2], recv_sem=t.rfy.at[k], device_id=ynbr, device_id_type=MESH).start()
+
+    def second_hop(k, t):
+        h = t.h
+        arrived(t.first_x.at[k], t.rfx.at[k])
+        t.own[k, 1 - y, x, :h] += t.half[k, 1 - y, x, :h] + t.first_x[k, 1 - y]
+        pltpu.make_async_remote_copy(
+            src_ref=t.own.at[k, 1 - y, x, pl.ds(0, h)], dst_ref=t.second_x.at[k],
+            send_sem=t.snd.at[3], recv_sem=t.rgx.at[k], device_id=ynbr, device_id_type=MESH).start()
+        arrived(t.first_y.at[k], t.rfy.at[k])
+        t.own[k, y, 1 - x, h:] += t.half[k, y, 1 - x, h:] + t.first_y[k, 1 - x]
+        pltpu.make_async_remote_copy(
+            src_ref=t.own.at[k, y, 1 - x, pl.ds(h, h)], dst_ref=t.second_y.at[k],
+            send_sem=t.snd.at[4], recv_sem=t.rgy.at[k], device_id=xnbr, device_id_type=MESH).start()
+
+    def finish(k, t, is_emb):
+        h = t.h
+        arrived(t.second_x.at[k], t.rgx.at[k])
+        t.own[k, y, x, :h] += t.half[k, y, x, :h] + t.first_x[k, y] + t.second_x[k]
+        arrived(t.second_y.at[k], t.rgy.at[k])
+        t.own[k, y, x, h:] += t.half[k, y, x, h:] + t.first_y[k, x] + t.second_y[k]
+        span = pl.ds(pl.multiple_of(k * CHUNK, CHUNK), CHUNK)
+        dst = t.out.at[span] if is_emb else t.out.at[:, span]
+        pltpu.make_async_copy(t.own.at[k, y, x], dst, t.osem.at[0]).start()
+
+    for k in range(AHEAD):
+        load(k, True)
+
+    barrier = pltpu.get_barrier_semaphore()
+    for peer in (partner, xnbr, ynbr):
+        pl.semaphore_signal(barrier, inc=1, device_id=peer, device_id_type=MESH)
+    pl.semaphore_wait(barrier, 3)
+
+    for k in range(AHEAD):
+        exchange(k, True)
+
+    total = 2 * steps
+
+    def both(k, act):
+        @pl.when((k >= 0) & (k < steps))
+        def _():
+            act(k, emb, True)
+
+        @pl.when((k >= steps) & (k < total))
+        def _():
+            act(k - steps, head, False)
+
+    def fetch(k, t, is_emb):
+        load(k, is_emb)
+        exchange(k, is_emb)
+
+    def step(i, carry):
+        both(i + AHEAD, fetch)
+        both(i, lambda k, t, is_emb: first_hop(k, t))
+        both(i - 1, lambda k, t, is_emb: second_hop(k, t))
+        both(i - 3, finish)
+        return carry
+
+    lax.fori_loop(0, total + 3, step, 0)
+
+    for t in (emb, head):
+        arrived(t.half, t.snd.at[0])
+        arrived(t.first_x, t.snd.at[1])
+        arrived(t.first_y, t.snd.at[2])
+        arrived(t.second_x, t.snd.at[3])
+        arrived(t.second_y, t.snd.at[4])
+        arrived(t.out, t.osem.at[0])
+
+
+def reduce_tables(emb_grad, head_grad):
+    rows, embed = emb_grad.shape
+    steps = rows // CHUNK
+    head_view = head_grad.reshape(2, 2, 2, LANES, rows)
+
+    def buffers(a, b):
+        return [pltpu.VMEM((steps, 2, 2, a, b), jnp.float32), pltpu.VMEM((steps, 2, 2, a, b), jnp.float32),
+                pltpu.VMEM((steps, 2, a // 2, b), jnp.float32), pltpu.VMEM((steps, 2, a // 2, b), jnp.float32),
+                pltpu.VMEM((steps, a // 2, b), jnp.float32), pltpu.VMEM((steps, a // 2, b), jnp.float32)]
+
+    sems = [pltpu.SemaphoreType.DMA((steps,)) for _ in range(6)]
+    sems += [pltpu.SemaphoreType.DMA((5,)), pltpu.SemaphoreType.DMA((1,))]
+    return pl.pallas_call(
+        functools.partial(reduce_kernel, steps),
+        out_shape=(jax.ShapeDtypeStruct((rows, LANES), jnp.float32), jax.ShapeDtypeStruct((LANES, rows), jnp.float32)),
+        in_specs=[pl.BlockSpec(memory_space=pl.ANY)] * 2,
+        out_specs=[pl.BlockSpec(memory_space=pl.ANY)] * 2,
+        scratch_shapes=buffers(CHUNK, LANES) + buffers(LANES, CHUNK) + sems + sems,
+        compiler_params=pltpu.CompilerParams(collective_id=0, has_side_effects=True, vmem_limit_bytes=60 * 1024 * 1024),
+    )(emb_grad, head_view)
 
 
 def apply_step(param, grad_sum, row_old, col_old, row_sq, col_sq, vocab_axis, vocab, embed):
@@ -45,8 +213,7 @@
         embed = emb_param.shape[1]
 
         def local_step(emb_block, head_block, emb_contrib, head_contrib, emb_rows, emb_cols, head_rows, head_cols):
-            emb_sum = lax.psum_scatter(emb_contrib[0], "data", scatter_dimension=1, tiled=True)
-            head_sum = lax.psum_scatter(head_contrib[0], "data", scatter_dimension=0, tiled=True)
+            emb_sum, head_sum = reduce_tables(emb_contrib[0], head_contrib[0])
             emb_new, emb_row_new, emb_col_new = block_update(emb_block, emb_sum, emb_rows, emb_cols, 0, vocab, embed)
             head_new, head_row_new, head_col_new = block_update(head_block, head_sum, head_rows, head_cols, 1, vocab, embed)
             return (emb_new, head_new, emb_row_new, emb_col_new, head_row_new, head_col_new,

time: 347 us -> 243 us (0.70)
  waiting for transfers between devices: 236 us -> 0 us
  Pallas kernels: 0 us -> 145 us
  between operations: 18.3 us -> 4.97 us
    reduce_scatter x2 -> x0, waiting for transfers between devices: 234 us -> none  [the longest x1 117 us: local_step(): lax.psum_scatter(head_contrib[0], 'data', scatter_dimension=0, tiled=True)]
    pallas_call x0 -> x1, Pallas kernels: none -> 145 us  [reduce_tables(): pl.pallas_call(functools.partial(reduce_kernel, steps), out_shape=(jax.Sh...]
  transfers between devices with their start and end apart: 2 -> 0, of which waited for: 2 -> 0; matrix products, arithmetic and copies ran while one was open for 1% -> 0% of each run, Pallas kernels for 0% -> 0%
where the time goes in v1:
time: 243 us; the launch traced here: 241 us
  Pallas kernels  145 us (60%)
  blocking collectives  72.6 us (30%)
  other arithmetic  18.8 us (8%)
  between operations  4.97 us (2%)
    pallas_call x1, Pallas kernels, reduce_tables(): pl.pallas_call(functools.partial(reduce_kernel, steps), out_shape=(jax.Sh...  145 us
    psum x1, blocking collectives, apply_step(): lax.psum(jnp.sum(param * param), ('model', 'data')) / (vocab * embed)  37.5 us
    psum x1, blocking collectives, block_update(): row_sq = lax.psum(jnp.sum(grad_sq, axis=embed_axis), 'data')  22.5 us
    psum x1, blocking collectives, block_update(): col_sq = lax.psum(jnp.sum(grad_sq, axis=vocab_axis), 'model')  12.6 us

profile of v1, /device:TPU:0, one launch (start us, length us, event | category | flops | bytes accessed | tf_op | source)
XLA Modules:
  0.0 241.2 jit_solution(15210736224604214921)
XLA Ops:
  0.6 0.0 copy-start.1
  0.6 2.9 %multiply_reduce_fusion.1 = f32[]{:T(128)} fusion(f32[128,4096]{1,0:T(8,128)} %param.9), kind=kLoop, calls=%fused_computation.4 | loop fusion | flops 1048575 | bytes 2097156 | tf_op jit(solution)/shard_map/reduce_sum | solution.py:192
  3.5 0.0 copy-done.1
  3.5 1.1 multiply_reduce_fusion.3
  4.7 144.8 %shard_map.143 = (f32[4096,128]{1,0:T(8,128)}, f32[128,4096]{1,0:T(8,128)}) custom-call(f32[4096,1024]{1,0:T(8,128)} %bitcast.2, f32[2,2,2,128,4096]{4,3,2,1,0:T(8,128)} %bitcast.3), custom_call_target="tpu_custom_call" | custom-call | tf_op jit(solution)/shard_map/pallas_call | solution.py:173
  149.4 0.0 copy-start
  149.5 0.0 copy-start.5
  149.5 0.0 copy-start.6
  149.5 0.0 copy-start.7
  149.5 2.4 fusion.1
  151.8 0.0 copy-done
  151.8 0.0 copy-start.8
  151.9 0.4 fusion.3
  152.2 22.5 %all-reduce.1 = (f32[4096]{0:T(1024)S(1)}, f32[4096]{0:T(1024)S(1)}) all-reduce(f32[4096]{0:T(1024)S(1)} %get-tuple-element.14, f32[4096]{0:T(1024)S(1)} %get-tuple-element.12), channel_id=1, replica_groups=mesh['model'=4,'data'=8] {'data'}, use_global_device_ids=true, to_apply=%region_3.0 | all-reduce | flops 8192 | bytes 65536 | tf_op jit(solution)/shard_map/psum | solution.py:200
  174.8 0.0 copy-done.5
  174.8 0.0 copy-done.6
  174.8 0.0 copy-start.3
  174.8 0.0 copy-start.4
  174.8 0.6 reduce_sum.93
  175.4 0.6 reduce_sum.98
  176.0 12.6 %all-reduce.2 = (f32[128]{0:T(128)S(1)}, f32[]{:T(128)}, f32[128]{0:T(128)S(1)}, f32[]{:T(128)}) all-reduce(f32[128]{0:T(128)S(1)} %get-tuple-element.15, f32[]{:T(128)} %reduce_sum.93, f32[128]{0:T(128)S(1)} %get-tuple-element.13, f32[]{:T(128)} %reduce_sum.98), channel_id=1, replica_groups=mesh['model'=4,'data'=8] {'model'}, use_global_device_ids=true, to_apply=%region_5.0 | all-reduce | flops 258 | bytes 2064 | tf_op jit(solution)/shard_map/psum | solution.py:201
  190.0 0.0 copy-done.7
  190.0 0.5 rsqrt_multiply_fusion.1
  190.5 2.5 %multiply_reduce_fusion.2 = f32[]{:T(128)} fusion(f32[4096,128]{1,0:T(8,128)} %get-tuple-element.10, f32[128]{0:T(128)S(1)} %get-tuple-element.36, f32[4096]{0:T(1024)S(1)} %get-tuple-element.38), kind=kLoop, calls=%fused_computation.6 | loop fusion | flops 2097151 | bytes 2114052 | tf_op jit(solution)/shard_map/reduce_sum | solution.py:191
  193.1 0.0 copy-done.8
  193.1 0.5 rsqrt_multiply_fusion
  193.6 1.3 multiply_reduce_fusion
  194.8 0.0 copy-done.3
  194.9 0.0 copy-done.4
  194.9 37.5 %all-reduce = (f32[]{:T(128)}, f32[]{:T(128)}, f32[]{:T(128)}, f32[]{:T(128)}) all-reduce(f32[]{:T(128)} %multiply_reduce_fusion.3, f32[]{:T(128)} %multiply_reduce_fusion.2, f32[]{:T(128)} %multiply_reduce_fusion.1, f32[]{:T(128)} %multiply_reduce_fusion), channel_id=1, replica_groups=mesh['model'=4,'data'=8] {'model','data'}, use_global_device_ids=true, to_apply=%region_1.0 | all-reduce | flops 4 | bytes 32 | tf_op jit(solution)/shard_map/psum | solution.py:192
  235.2 0.0 copy-start.2
  235.2 3.8 %fusion.5 = (bf16[4096,128]{1,0:T(8,128)(2,1)}, f32[4096,128]{1,0:T(8,128)}) fusion(f32[4096,128]{1,0:T(8,128)} %param.8, f32[128]{0:T(128)S(1)} %get-tuple-element.36, f32[4096,128]{1,0:T(8,128)} %get-tuple-element.10, f32[4096]{0:T(1024)S(1)} %get-tuple-element.38, f32[]{:T(128)S(6)} %div.33), kind=kLoop, calls=%fused_computation.21 | loop fusion | flops 2621440 | bytes 7356932 | tf_op jit(solution)/shard_map/convert_element_type | solution.py:220
  239.0 0.0 copy-done.2
  239.0 2.2 fusion.4
  (1 shorter events, 0.0 us)
Async XLA Ops:
  0.6 2.9 %copy-start.1 = (f32[4096,128]{1,0:T(8,128)S(1)}, f32[4096,128]{1,0:T(8,128)}, u32[]{:S(2)}) copy-start(f32[4096,128]{1,0:T(8,128)} %param.8) | copy-start | bytes 6291460
  149.4 2.4 copy-start
  149.5 25.3 %copy-start.5 = (f32[4096]{0:T(1024)S(1)}, f32[4096]{0:T(1024)}, u32[]{:S(2)}) copy-start(f32[4096]{0:T(1024)} %param.14) | copy-start | bytes 49156
  149.5 25.3 %copy-start.6 = (f32[4096]{0:T(1024)S(1)}, f32[4096]{0:T(1024)}, u32[]{:S(2)}) copy-start(f32[4096]{0:T(1024)} %param.12) | copy-start | bytes 49156
  149.5 40.5 %copy-start.7 = (f32[128]{0:T(128)S(1)}, f32[128]{0:T(128)}, u32[]{:S(2)}) copy-start(f32[128]{0:T(128)} %param.13) | copy-start | bytes 1540
  151.8 41.2 %copy-start.8 = (f32[128]{0:T(128)S(1)}, f32[128]{0:T(128)}, u32[]{:S(2)}) copy-start(f32[128]{0:T(128)} %param.15) | copy-start | bytes 1540
  174.8 20.0 %copy-start.3 = (f32[4096]{0:T(1024)}, f32[4096]{0:T(1024)S(1)}, u32[]{:S(2)}) copy-start(f32[4096]{0:T(1024)S(1)} %get-tuple-element.31) | copy-start | bytes 49156
  174.8 20.0 %copy-start.4 = (f32[4096]{0:T(1024)}, f32[4096]{0:T(1024)S(1)}, u32[]{:S(2)}) copy-start(f32[4096]{0:T(1024)S(1)} %get-tuple-element.39) | copy-start | bytes 49156
  235.2 3.8 %copy-start.2 = (f32[128,4096]{1,0:T(8,128)S(1)}, f32[128,4096]{1,0:T(8,128)}, u32[]{:S(2)}) copy-start(f32[128,4096]{1,0:T(8,128)} %param.9) | copy-start | bytes 6291460

commit v2 on v0

v2 whole, which is shorter than its diff:
```python
import functools

import jax
import jax.numpy as jnp
from jax import lax
from jax.experimental import pallas as pl
from jax.experimental.pallas import tpu as pltpu
from jax.sharding import PartitionSpec as P

TRAIN_STEP = 10
DECAY_EXP = 0.8
EPS_ONE = 1e-30
CLIP_LIMIT = 1.0
SCALE_FLOOR = 1e-3
LEARN_RATE = float(TRAIN_STEP) ** -0.5
BETA_TWO = 1.0 - float(TRAIN_STEP) ** -DECAY_EXP

MESH = pl.DeviceIdType.MESH
CHUNK = 256
AHEAD = 3
LANES = 128
VMEM_MIB = 54


class Table:
    def __init__(self, is_emb, grad, param, row, col, outs, bufs, small, sems):
        self.is_emb, self.grad, self.param, self.row, self.col = is_emb, grad, param, row, col
        self.dirn, self.pcopy, self.row_new, self.col_new, self.scale = outs
        self.own, self.half, self.first_x, self.first_y, self.second_x, self.second_y = bufs
        self.rpart, self.rrecv, self.col_acc, self.w_acc, self.r_acc, self.p_acc, self.colx, self.scalx, self.vec = small
        (self.ld, self.ra, self.rfx, self.rfy, self.rgx, self.rgy, self.rr0, self.rr1, self.rr2, self.snd, self.one) = sems
        self.rr = (self.rr0, self.rr1, self.rr2)
        self.h = (CHUNK if is_emb else LANES) // 2


N_OUT, N_BUF, N_SMALL, N_SEM = 5, 6, 9, 11


def arrived(ref, sem):
    pltpu.make_async_copy(ref, ref, sem).wait()


def lane_sum(a):
    return jnp.sum(a, axis=1, keepdims=True)


def fold8(a):
    return jnp.sum(a.reshape(a.shape[0] // 8, 8, a.shape[1]), axis=0)


def adafactor_kernel(steps, nz, nd, *refs):
    emb_in, head_in = refs[0:4], refs[4:8]
    pos = 8
    emb_out, head_out = refs[pos:pos + N_OUT], refs[pos + N_OUT:pos + 2 * N_OUT]
    pos += 2 * N_OUT
    emb_buf, head_buf = refs[pos:pos + N_BUF], refs[pos + N_BUF:pos + 2 * N_BUF]
    pos += 2 * N_BUF
    emb_small, head_small = refs[pos:pos + N_SMALL], refs[pos + N_SMALL:pos + 2 * N_SMALL]
    pos += 2 * N_SMALL
    emb_sem, head_sem = refs[pos:pos + N_SEM], refs[pos + N_SEM:pos + 2 * N_SEM]
    emb = Table(True, *emb_in, emb_out, emb_buf, emb_small, emb_sem)
    head = Table(False, *head_in, head_out, head_buf, head_small, head_sem)
    vocab, embed = float(nz * steps * CHUNK), float(nd * LANES)
    others = nz * nd - 1

    z = lax.axis_index("model")
    d = lax.axis_index("data")
    me = z * nd + d
    c = lax.rem(d, 2)
    x = lax.rem(d // 2, 2)
    y = d // 4
    partner = (z, d + 1 - 2 * c)
    xnbr = (z, d + 2 - 4 * x)
    ynbr = (z, d + 4 - 8 * y)
    ring = (partner, xnbr, ynbr)

    def emb_slice(k, yy, xx, core):
        col = pl.multiple_of(((yy * 2 + xx) * 2 + core) * LANES, LANES)
        return emb.grad.at[pl.ds(pl.multiple_of(k * CHUNK, CHUNK), CHUNK), pl.ds(col, LANES)]

    def head_slice(k, core):
        return head.grad.at[:, :, core, :, pl.ds(pl.multiple_of(k * CHUNK, CHUNK), CHUNK)]

    def send(src, dst, ssem, rsem, to):
        pltpu.make_async_remote_copy(src_ref=src, dst_ref=dst, send_sem=ssem, recv_sem=rsem,
                                     device_id=to, device_id_type=MESH).start()

    def load(k, t):
        if t.is_emb:
            for yy in range(2):
                for xx in range(2):
                    pltpu.make_async_copy(emb_slice(k, yy, xx, c), t.own.at[k, yy, xx], t.ld.at[k]).start()
        else:
            pltpu.make_async_copy(head_slice(k, c), t.own.at[k], t.ld.at[k]).start()

    def exchange(k, t):
        if t.is_emb:
            for yy in range(2):
                for xx in range(2):
                    send(emb_slice(k, yy, xx, 1 - c), t.half.at[k, yy, xx], t.snd.at[0], t.ra.at[k], partner)
        else:
            send(head_slice(k, 1 - c), t.half.at[k], t.snd.at[0], t.ra.at[k], partner)

    def first_hop(k, t):
        arrived(t.own.at[k], t.ld.at[k])
        arrived(t.half.at[k], t.ra.at[k])
        h = t.h
        for yy in range(2):
            t.own[k, yy, 1 - x, :h] += t.half[k, yy, 1 - x, :h]
        send(t.own.at[k, :, 1 - x, pl.ds(0, h)], t.first_x.at[k], t.snd.at[1], t.rfx.at[k], xnbr)
        for xx in range(2):
            t.own[k, 1 - y, xx, h:] += t.half[k, 1 - y, xx, h:]
        send(t.own.at[k, 1 - y, :, pl.ds(h, h)], t.first_y.at[k], t.snd.at[2], t.rfy.at[k], ynbr)

    def second_hop(k, t):
        h = t.h
        arrived(t.first_x.at[k], t.rfx.at[k])
        t.own[k, 1 - y, x, :h] += t.half[k, 1 - y, x, :h] + t.first_x[k, 1 - y]
        send(t.own.at[k, 1 - y, x, pl.ds(0, h)], t.second_x.at[k], t.snd.at[3], t.rgx.at[k], ynbr)
        arrived(t.first_y.at[k], t.rfy.at[k])
        t.own[k, y, 1 - x, h:] += t.half[k, y, 1 - x, h:] + t.first_y[k, 1 - x]
        send(t.own.at[k, y, 1 - x, pl.ds(h, h)], t.second_y.at[k], t.snd.at[4], t.rgy.at[k], xnbr)

    def tile(k, i):
        return pl.ds(pl.multiple_of(k * CHUNK + i * LANES, LANES), LANES)

    def finish(k, t):
        h = t.h
        arrived(t.second_x.at[k], t.rgx.at[k])
        arrived(t.second_y.at[k], t.rgy.at[k])
        first = t.own[k, y, x, :h] + t.half[k, y, x, :h] + t.first_x[k, y] + t.second_x[k]
        last = t.own[k, y, x, h:] + t.half[k, y, x, h:] + t.first_y[k, x] + t.second_y[k]
        if t.is_emb:
            for i, g in enumerate((first, last)):
                t.dirn[tile(k, i), :] = g
                sq = g * g + EPS_ONE
                t.col_acc[...] += fold8(sq)
                t.rpart[0, k, i:i + 1, :] = jnp.sum(jnp.transpose(sq), axis=0, keepdims=True)
                p = t.pcopy[tile(k, i), :]
                t.p_acc[...] += fold8(p * p)
        else:
            for i in range(CHUNK // LANES):
                lanes = slice(i * LANES, (i + 1) * LANES)
                t.dirn[:h, tile(k, i)] = first[:, lanes]
                t.dirn[h:, tile(k, i)] = last[:, lanes]
                sq_first = first[:, lanes] * first[:, lanes] + EPS_ONE
                sq_last = last[:, lanes] * last[:, lanes] + EPS_ONE
                t.col_acc[:h] += sq_first
                t.col_acc[h:] += sq_last
                t.rpart[0, k, i:i + 1, :] = jnp.sum(fold8(sq_first) + fold8(sq_last), axis=0, keepdims=True)
                p = t.pcopy[:, tile(k, i)]
                t.p_acc[...] += fold8(p * p)
        send(t.rpart.at[0, k], t.rrecv.at[0, k], t.snd.at[5], t.rr[0].at[k], ring[0])

    def row_hop(s, k, t):
        arrived(t.rrecv.at[s - 1, k], t.rr[s - 1].at[k])
        t.rpart[s, k] = t.rpart[s - 1, k] + t.rrecv[s - 1, k]
        send(t.rpart.at[s, k], t.rrecv.at[s, k], t.snd.at[5 + s], t.rr[s].at[k], ring[s])

    def complete(k, t):
        arrived(t.rrecv.at[2, k], t.rr[2].at[k])
        row_sq = t.rpart[2, k] + t.rrecv[2, k]
        rows = pl.ds(k * (CHUNK // LANES), CHUNK // LANES)
        new = BETA_TWO * t.row[rows, :] + (1.0 - BETA_TWO) * (row_sq / embed)
        t.row_new[rows, :] = new
        t.r_acc[...] += new
        factor = lax.rsqrt(new)
        for i in range(CHUNK // LANES):
            line = jnp.broadcast_to(factor[i:i + 1, :], (LANES, LANES))
            if t.is_emb:
                n = t.dirn[tile(k, i), :] * jnp.transpose(line)
                t.dirn[tile(k, i), :] = n
                t.w_acc[...] += fold8(n * n)
            else:
                n = t.dirn[:, tile(k, i)] * line
                t.dirn[:, tile(k, i)] = n
                t.w_acc[...] += n * n

    def per_col(t, acc):
        a = acc[...]
        return jnp.sum(a if t.is_emb else jnp.transpose(a), axis=0, keepdims=True)

    def send_cols(t):
        t.vec[0] = per_col(t, t.col_acc)
        for o in range(1, nz):
            send(t.vec.at[0], t.colx.at[z], t.one.at[0], t.one.at[1], (lax.rem(z + o, nz), d))

    def send_scalars(t):
        arrived(t.colx.at[pl.ds(0, nz - 1)], t.one.at[1])
        t.colx[z] = t.vec[0]
        col_sq = t.colx[0]
        for i in range(1, nz):
            col_sq = col_sq + t.colx[i]
        new = BETA_TWO * t.col[...] + (1.0 - BETA_TWO) * (col_sq / vocab)
        t.col_new[...] = new
        w = lane_sum(per_col(t, t.w_acc) / new)
        r = lane_sum(jnp.sum(t.r_acc[...], axis=0, keepdims=True)) / nd
        p = lane_sum(jnp.sum(t.p_acc[...], axis=0, keepdims=True))
        lane = lax.broadcasted_iota(jnp.int32, (1, LANES), 1)
        t.vec[1] = jnp.where(lane == 0, w, jnp.where(lane == 1, r, jnp.where(lane == 2, p, 0.0)))

        def one(o, carry):
            to = lax.rem(me + o, others + 1)
            send(t.vec.at[1], t.scalx.at[me], t.one.at[2], t.one.at[3], (to // nd, lax.rem(to, nd)))
            return carry

        lax.fori_loop(1, others + 1, one, 0)

    def finish_scalars(t):
        arrived(t.scalx.at[pl.ds(0, others)], t.one.at[3])
        t.scalx[me] = t.vec[1]
        total = jnp.sum(t.scalx[...], axis=0)
        lane = lax.broadcasted_iota(jnp.int32, (1, LANES), 1)
        w, r, p = (lane_sum(jnp.where(lane == i, total, 0.0)) for i in range(3))
        row_mean = r / vocab
        update_rms = jnp.sqrt(w * row_mean / (vocab * embed))
        param_rms = jnp.sqrt(p / (vocab * embed))
        step_size = LEARN_RATE * jnp.maximum(SCALE_FLOOR, param_rms) / jnp.maximum(1.0, update_rms / CLIP_LIMIT)
        line = lax.rsqrt(t.col_new[...]) * (jnp.sqrt(row_mean) * step_size)
        if t.is_emb:
            t.scale[...] = jnp.broadcast_to(line, t.scale.shape)
        else:
            t.scale[...] = jnp.transpose(jnp.broadcast_to(line, (LANES, LANES)))

    for k in range(AHEAD):
        load(k, emb)
    for t in (emb, head):
        pltpu.make_async_copy(t.param, t.pcopy, t.one.at[4]).start()
        for acc in (t.col_acc, t.w_acc, t.r_acc, t.p_acc):
            acc[...] = jnp.zeros_like(acc)

    barrier = pltpu.get_barrier_semaphore()

    def greet(o, carry):
        to = lax.rem(me + o, others + 1)
        pl.semaphore_signal(barrier, inc=1, device_id=(to // nd, lax.rem(to, nd)), device_id_type=MESH)
        return carry

    lax.fori_loop(1, others + 1, greet, 0)
    pl.semaphore_wait(barrier, others)

    for k in range(AHEAD):
        exchange(k, emb)
    for t in (emb, head):
        arrived(t.pcopy, t.one.at[4])

    total = 2 * steps

    def both(k, act):
        @pl.when((k >= 0) & (k < steps))
        def _():
            act(k, emb)

        @pl.when((k >= steps) & (k < total))
        def _():
            act(k - steps, head)

    def fetch(k, t):
        load(k, t)
        exchange(k, t)

    def step(i, carry):
        both(i + AHEAD, fetch)
        both(i, first_hop)
        both(i - 1, second_hop)
        both(i - 3, finish)

        @pl.when(i == steps + 2)
        def _():
            send_cols(emb)

        @pl.when(i == total + 2)
        def _():
            send_cols(head)

        both(i - 4, functools.partial(row_hop, 1))
        both(i - 6, functools.partial(row_hop, 2))
        both(i - 8, complete)

        @pl.when(i == steps + 8)
        def _():
            send_scalars(emb)

        @pl.when(i == steps + 11)
        def _():
            finish_scalars(emb)

        return carry

    lax.fori_loop(0, total + 8, step, 0)
    send_scalars(head)
    finish_scalars(head)

    for t in (emb, head):
        arrived(t.half, t.snd.at[0])
        arrived(t.first_x, t.snd.at[1])
        arrived(t.first_y, t.snd.at[2])
        arrived(t.second_x, t.snd.at[3])
        arrived(t.second_y, t.snd.at[4])
        for s in range(3):
            arrived(t.rpart.at[s], t.snd.at[5 + s])
        arrived(t.colx.at[pl.ds(0, nz - 1)], t.one.at[0])
        arrived(t.scalx.at[pl.ds(0, others)], t.one.at[2])


def statistics(mesh, emb_grad, head_grad, emb_param, head_param, emb_row, emb_col, head_row, head_col):
    rows = emb_grad.shape[0]
    steps = rows // CHUNK
    nz, nd = mesh.shape["model"], mesh.shape["data"]
    f32 = jnp.float32

    def buffers(a, b):
        return [pltpu.VMEM((steps, 2, 2, a, b), f32), pltpu.VMEM((steps, 2, 2, a, b), f32),
                pltpu.VMEM((steps, 2, a // 2, b), f32), pltpu.VMEM((steps, 2, a // 2, b), f32),
                pltpu.VMEM((steps, a // 2, b), f32), pltpu.VMEM((steps, a // 2, b), f32)]

    def small(acc_rows):
        per = CHUNK // LANES
        return [pltpu.VMEM((3, steps, per, LANES), f32), pltpu.VMEM((3, steps, per, LANES), f32),
                pltpu.VMEM((acc_rows, LANES), f32), pltpu.VMEM((acc_rows, LANES), f32),
                pltpu.VMEM((per, LANES), f32), pltpu.VMEM((8, LANES), f32),
                pltpu.VMEM((nz, 1, LANES), f32), pltpu.VMEM((nz * nd, 1, LANES), f32), pltpu.VMEM((2, 1, LANES), f32)]

    sems = [pltpu.SemaphoreType.DMA((steps,)) for _ in range(9)]
    sems += [pltpu.SemaphoreType.DMA((8,)), pltpu.SemaphoreType.DMA((5,))]

    def outs(shape, scale_rows):
        return [jax.ShapeDtypeStruct(shape, f32), jax.ShapeDtypeStruct(shape, f32),
                jax.ShapeDtypeStruct((rows // LANES, LANES), f32), jax.ShapeDtypeStruct((1, LANES), f32),
                jax.ShapeDtypeStruct((scale_rows, LANES), f32)]

    anyspace = pl.BlockSpec(memory_space=pl.ANY)
    vmem = pl.BlockSpec(memory_space=pltpu.VMEM)
    results = pl.pallas_call(
        functools.partial(adafactor_kernel, steps, nz, nd),
        out_shape=outs((rows, LANES), 8) + outs((LANES, rows), LANES),
        in_specs=[anyspace, anyspace, vmem, vmem] * 2,
        out_specs=[vmem] * 10,
        scratch_shapes=(buffers(CHUNK, LANES) + buffers(LANES, CHUNK) + small(8) + small(LANES) + sems + sems),
        compiler_params=pltpu.CompilerParams(collective_id=0, has_side_effects=True, vmem_limit_bytes=VMEM_MIB * 2 ** 20),
    )(emb_grad, emb_param, emb_row.reshape(rows // LANES, LANES), emb_col.reshape(1, LANES),
      head_grad.reshape(2, 2, 2, LANES, rows), head_param, head_row.reshape(rows // LANES, LANES),
      head_col.reshape(1, LANES))
    return results[:5], results[5:]


PIECES = 8


def apply_kernel(rows, *refs):
    (emb_dir, emb_p, emb_r, emb_c, emb_s, head_dir, head_p, head_r, head_c, head_s,
     emb_new, emb_b16, head_new, head_b16, emb_ro, emb_co, head_ro, head_co,
     emb_tmp, emb_tmp16, head_tmp, head_tmp16, sem) = refs
    size = rows // PIECES

    def piece(j, carry):
        span = pl.ds(pl.multiple_of(j * size, size), size)
        new = emb_p[span, :] - emb_dir[span, :] * emb_s[0:1, :]
        emb_tmp[span, :] = new
        emb_tmp16[span, :] = new.astype(jnp.bfloat16)
        pltpu.make_async_copy(emb_tmp.at[span], emb_new.at[span], sem.at[0]).start()
        pltpu.make_async_copy(emb_tmp16.at[span], emb_b16.at[span], sem.at[1]).start()
        for i in range(size // LANES):
            cols = pl.ds(pl.multiple_of(j * size + i * LANES, LANES), LANES)
            new = head_p[:, cols] - head_dir[:, cols] * head_s[...]
            head_tmp[:, cols] = new
            head_tmp16[:, cols] = new.astype(jnp.bfloat16)
        pltpu.make_async_copy(head_tmp.at[:, span], head_new.at[:, span], sem.at[2]).start()
        pltpu.make_async_copy(head_tmp16.at[:, span], head_b16.at[:, span], sem.at[3]).start()
        return carry

    emb_ro[...] = emb_r[...]
    emb_co[...] = emb_c[...]
    head_ro[...] = head_r[...]
    head_co[...] = head_c[...]
    lax.fori_loop(0, PIECES, piece, 0)
    arrived(emb_new, sem.at[0])
    arrived(emb_b16, sem.at[1])
    arrived(head_new, sem.at[2])
    arrived(head_b16, sem.at[3])


def apply_update(emb, head):
    rows = emb[0].shape[0]
    f32, b16 = jnp.float32, jnp.bfloat16
    anyspace = pl.BlockSpec(memory_space=pl.ANY)
    vmem = pl.BlockSpec(memory_space=pltpu.VMEM)
    shapes = ((rows, LANES), f32), ((rows, LANES), b16), ((LANES, rows), f32), ((LANES, rows), b16)
    small = ((rows // LANES, LANES), f32), ((1, LANES), f32)
    emb_new, emb_b16, head_new, head_b16, emb_r, emb_c, head_r, head_c = pl.pallas_call(
        functools.partial(apply_kernel, rows),
        out_shape=[jax.ShapeDtypeStruct(s, t) for s, t in shapes + small + small],
        in_specs=[vmem] * 10,
        out_specs=[anyspace] * 4 + [vmem] * 4,
        scratch_shapes=[pltpu.VMEM(s, t) for s, t in shapes] + [pltpu.SemaphoreType.DMA((4,))],
        compiler_params=pltpu.CompilerParams(vmem_limit_bytes=24 * 2 ** 20),
    )(*emb, *head)
    return (emb_new, head_new, emb_r.reshape(rows), emb_c.reshape(LANES), head_r.reshape(rows), head_c.reshape(LANES),
            emb_b16, head_b16)


def solution(mesh):
    arg_specs = (P("model", "data"), P("data", "model"), P("data", "model", None), P("data", None, "model"),
                 P("model"), P("data"), P("model"), P("data"))
    result_specs = (P("model", "data"), P("data", "model"), P("model"), P("data"), P("model"), P("data"),
                    P("model", "data"), P("data", "model"))

    def local_step(emb_block, head_block, emb_contrib, head_contrib, emb_rows, emb_cols, head_rows, head_cols):
        emb, head = statistics(mesh, emb_contrib[0], head_contrib[0], emb_block, head_block,
                               emb_rows, emb_cols, head_rows, head_cols)
        return apply_update(emb, head)

    return jax.shard_map(local_step, mesh=mesh, in_specs=arg_specs, out_specs=result_specs, check_vma=False)
```

time: 347 us -> 179 us (0.52)
  waiting for transfers between devices: 236 us -> 0 us
  Pallas kernels: 0 us -> 168 us
  blocking collectives: 72.3 us -> 0 us
  other arithmetic: 18.5 us -> 0 us
  between operations: 18.3 us -> 0.66 us
  local copies, waits for them, and re-layouts: 1.39 us -> 10.5 us
    reduce_scatter x2 -> x0, waiting for transfers between devices: 234 us -> none  [the longest x1 117 us: local_step(): lax.psum_scatter(head_contrib[0], 'data', scatter_dimension=0, tiled=True)]
    pallas_call x0 -> x2, Pallas kernels: none -> 168 us  [the longest x1 164 us: statistics(): pl.pallas_call(functools.partial(adafactor_kernel, steps, nz, nd), out_sh...]
    psum x3 -> x0, blocking collectives: 72.3 us -> none  [the longest x1 37.2 us: apply_step(): lax.psum(jnp.sum(param * param), ('model', 'data')) / (vocab * embed)]
    reduce_sum x8 -> x0, other arithmetic: 11.4 us -> none  [the longest x2 4.17 us: block_update(): row_sq = lax.psum(jnp.sum(grad_sq, axis=embed_axis), 'data')]
    unnamed x20, local copies, waits for them, and re-layouts: 1.39 us -> 10.5 us
    convert_element_type x2 -> x0, other arithmetic: 5.96 us -> none  [the longest x1 3.81 us: local_step(): emb_new.astype(jnp.bfloat16)]
  transfers between devices with their start and end apart: 2 -> 0, of which waited for: 2 -> 0; matrix products, arithmetic and copies ran while one was open for 1% -> 0% of each run, Pallas kernels for 0% -> 0%
where the time goes in v2:
time: 179 us
  Pallas kernels  168 us (94%)
  local copies, waits for them, and re-layouts  10.5 us (6%)
    pallas_call x1, Pallas kernels, statistics(): pl.pallas_call(functools.partial(adafactor_kernel, steps, nz, nd), out_sh...  164 us
    unnamed x20, local copies, waits for them, and re-layouts  10.5 us

profile of v2, /device:TPU:0, one launch (start us, length us, event | category | flops | bytes accessed | tf_op | source)
XLA Modules:
  0.0 178.7 jit_solution(10093919094911994648)
XLA Ops:
  0.6 164.2 %shard_map.143 = (f32[4096,128]{1,0:T(8,128)}, f32[4096,128]{1,0:T(8,128)}, f32[32,128]{1,0:T(8,128)}, f32[1,128]{1,0:T(1,128)}, f32[8,128]{1,0:T(8,128)}, /*ind...) custom-call(f32[4096,1024]{1,0:T(8,128)} %bitcast.10, ...), custom_call_target="tpu_custom_call" | custom-call | tf_op jit(solution)/shard_map/pallas_call | solution.py:334
  164.8 0.0 copy-start
  164.8 1.6 copy-done
  166.4 0.0 copy-start.1
  166.4 1.6 copy-done.1
  168.0 0.0 copy-start.2
  168.0 1.6 copy-done.2
  169.6 0.0 copy-start.3
  169.6 1.6 copy-done.3
  171.2 0.0 copy-start.4
  171.2 0.8 copy-done.4
  172.0 0.0 copy-start.5
  172.0 0.7 copy-done.5
  172.7 0.0 copy-start.6
  172.7 0.7 copy-done.6
  173.5 0.0 copy-start.7
  173.5 0.7 copy-done.7
  174.1 0.0 copy-start.8
  174.1 0.6 copy-done.8
  174.7 0.0 copy-start.9
  174.7 0.6 copy-done.9
  175.3 3.4 %shard_map.144 = (f32[4096,128]{1,0:T(8,128)}, bf16[4096,128]{1,0:T(8,128)(2,1)}, f32[128,4096]{1,0:T(8,128)}, bf16[128,4096]{1,0:T(8,128)(2,1)}, f32[32,128]{1,...) custom-call(f32[4096,128]{1,0:T(8,128)S(1)} %copy-done, f32[4096,128]{1,0:T(8,128)S(1)} %copy-done.1, ...), custom_call_target="tpu_custom_call" | custom-call | tf_op jit(solution)/shard_map/pallas_call | solution.py:390
Async XLA Ops:
  164.8 1.6 copy-start
  166.4 1.6 copy-start.1
  168.0 1.6 copy-start.2
  169.6 1.6 copy-start.3
  171.2 0.8 copy-start.4
  172.0 0.7 copy-start.5
  172.7 0.7 copy-start.6
  173.5 0.7 copy-start.7
  174.1 0.6 copy-start.8
  174.7 0.6 copy-start.9

commit v3 on v2

--- a/solution.py
+++ b/solution.py
@@ -19,21 +19,21 @@
 CHUNK = 256
 AHEAD = 3
 LANES = 128
-VMEM_MIB = 54
+VMEM_MIB = 45
 
 
 class Table:
-    def __init__(self, is_emb, grad, param, row, col, outs, bufs, small, sems):
-        self.is_emb, self.grad, self.param, self.row, self.col = is_emb, grad, param, row, col
+    def __init__(self, is_emb, grad, param, row_old, col_old, outs, bufs, small, sems):
+        self.is_emb, self.grad, self.param, self.row_old, self.col_old = is_emb, grad, param, row_old, col_old
         self.dirn, self.pcopy, self.row_new, self.col_new, self.scale = outs
         self.own, self.half, self.first_x, self.first_y, self.second_x, self.second_y = bufs
-        self.rpart, self.rrecv, self.col_acc, self.w_acc, self.r_acc, self.p_acc, self.colx, self.scalx, self.vec = small
+        self.rpart, self.rrecv, self.col_acc, self.w_acc, self.r_acc, self.p_acc, self.colx, self.scalx, self.vec, self.row, self.col = small
         (self.ld, self.ra, self.rfx, self.rfy, self.rgx, self.rgy, self.rr0, self.rr1, self.rr2, self.snd, self.one) = sems
         self.rr = (self.rr0, self.rr1, self.rr2)
         self.h = (CHUNK if is_emb else LANES) // 2
 
 
-N_OUT, N_BUF, N_SMALL, N_SEM = 5, 6, 9, 11
+N_OUT, N_BUF, N_SMALL, N_SEM = 5, 6, 11, 11
 
 
 def arrived(ref, sem):
@@ -225,7 +225,8 @@
     for k in range(AHEAD):
         load(k, emb)
     for t in (emb, head):
-        pltpu.make_async_copy(t.param, t.pcopy, t.one.at[4]).start()
+        for i, (src, dst) in enumerate(((t.param, t.pcopy), (t.row_old, t.row), (t.col_old, t.col))):
+            pltpu.make_async_copy(src, dst, t.one.at[4 + i]).start()
         for acc in (t.col_acc, t.w_acc, t.r_acc, t.p_acc):
             acc[...] = jnp.zeros_like(acc)
 
@@ -241,9 +242,6 @@
 
     for k in range(AHEAD):
         exchange(k, emb)
-    for t in (emb, head):
-        arrived(t.pcopy, t.one.at[4])
-
     total = 2 * steps
 
     def both(k, act):
@@ -263,6 +261,14 @@
         both(i + AHEAD, fetch)
         both(i, first_hop)
         both(i - 1, second_hop)
+
+        @pl.when(i == 2)
+        def _():
+            for t in (emb, head):
+                arrived(t.pcopy, t.one.at[4])
+                arrived(t.row, t.one.at[5])
+                arrived(t.col, t.one.at[6])
+
         both(i - 3, finish)
 
         @pl.when(i == steps + 2)
@@ -319,22 +325,23 @@
         return [pltpu.VMEM((3, steps, per, LANES), f32), pltpu.VMEM((3, steps, per, LANES), f32),
                 pltpu.VMEM((acc_rows, LANES), f32), pltpu.VMEM((acc_rows, LANES), f32),
                 pltpu.VMEM((per, LANES), f32), pltpu.VMEM((8, LANES), f32),
-                pltpu.VMEM((nz, 1, LANES), f32), pltpu.VMEM((nz * nd, 1, LANES), f32), pltpu.VMEM((2, 1, LANES), f32)]
+                pltpu.VMEM((nz, 1, LANES), f32), pltpu.VMEM((nz * nd, 1, LANES), f32), pltpu.VMEM((2, 1, LANES), f32),
+                pltpu.VMEM((rows // LANES, LANES), f32), pltpu.VMEM((1, LANES), f32)]
 
     sems = [pltpu.SemaphoreType.DMA((steps,)) for _ in range(9)]
-    sems += [pltpu.SemaphoreType.DMA((8,)), pltpu.SemaphoreType.DMA((5,))]
+    sems += [pltpu.SemaphoreType.DMA((8,)), pltpu.SemaphoreType.DMA((7,))]
 
     def outs(shape, scale_rows):
         return [jax.ShapeDtypeStruct(shape, f32), jax.ShapeDtypeStruct(shape, f32),
                 jax.ShapeDtypeStruct((rows // LANES, LANES), f32), jax.ShapeDtypeStruct((1, LANES), f32),
                 jax.ShapeDtypeStruct((scale_rows, LANES), f32)]
 
-    anyspace = pl.BlockSpec(memory_space=pl.ANY)
+    hbm = pl.BlockSpec(memory_space=pltpu.HBM)
     vmem = pl.BlockSpec(memory_space=pltpu.VMEM)
     results = pl.pallas_call(
         functools.partial(adafactor_kernel, steps, nz, nd),
         out_shape=outs((rows, LANES), 8) + outs((LANES, rows), LANES),
-        in_specs=[anyspace, anyspace, vmem, vmem] * 2,
+        in_specs=[hbm] * 8,
         out_specs=[vmem] * 10,
         scratch_shapes=(buffers(CHUNK, LANES) + buffers(LANES, CHUNK) + small(8) + small(LANES) + sems + sems),
         compiler_params=pltpu.CompilerParams(collective_id=0, has_side_effects=True, vmem_limit_bytes=VMEM_MIB * 2 ** 20),
@@ -383,7 +390,7 @@
 def apply_update(emb, head):
     rows = emb[0].shape[0]
     f32, b16 = jnp.float32, jnp.bfloat16
-    anyspace = pl.BlockSpec(memory_space=pl.ANY)
+    hbm = pl.BlockSpec(memory_space=pltpu.HBM)
     vmem = pl.BlockSpec(memory_space=pltpu.VMEM)
     shapes = ((rows, LANES), f32), ((rows, LANES), b16), ((LANES, rows), f32), ((LANES, rows), b16)
     small = ((rows // LANES, LANES), f32), ((1, LANES), f32)
@@ -391,7 +398,7 @@
         functools.partial(apply_kernel, rows),
         out_shape=[jax.ShapeDtypeStruct(s, t) for s, t in shapes + small + small],
         in_specs=[vmem] * 10,
-        out_specs=[anyspace] * 4 + [vmem] * 4,
+        out_specs=[hbm] * 4 + [vmem] * 4,
         scratch_shapes=[pltpu.VMEM(s, t) for s, t in shapes] + [pltpu.SemaphoreType.DMA((4,))],
         compiler_params=pltpu.CompilerParams(vmem_limit_bytes=24 * 2 ** 20),
     )(*emb, *head)

time: 179 us -> 167 us (0.933)
  local copies, waits for them, and re-layouts: 10.5 us -> 2.74 us
  Pallas kernels: 168 us -> 164 us
    unnamed x20 -> x8, local copies, waits for them, and re-layouts: 10.5 us -> 2.74 us
    pallas_call x1, Pallas kernels: 164 us -> 160 us  [statistics(): pl.pallas_call(functools.partial(adafactor_kernel, steps, nz, nd), out_sh...]
where the time goes in v3:
time: 167 us
  Pallas kernels  164 us (98%)
  local copies, waits for them, and re-layouts  2.74 us (2%)
    pallas_call x1, Pallas kernels, statistics(): pl.pallas_call(functools.partial(adafactor_kernel, steps, nz, nd), out_sh...  160 us
    pallas_call x1, Pallas kernels, apply_update(): pl.pallas_call(functools.partial(apply_kernel, rows), out_shape=[jax.Shap...  3.37 us

profile of v3, /device:TPU:0, one launch (start us, length us, event | category | flops | bytes accessed | tf_op | source)
XLA Modules:
  0.0 166.9 jit_solution(18209096854844600348)
XLA Ops:
  0.6 0.0 copy-start
  0.6 0.7 copy-done
  1.4 0.0 copy-start.1
  1.4 0.7 copy-done.1
  2.1 0.0 copy-start.2
  2.1 0.7 copy-done.2
  2.7 0.0 copy-start.3
  2.7 0.7 copy-done.3
  3.4 160.1 %shard_map.143 = (f32[4096,128]{1,0:T(8,128)S(1)}, f32[4096,128]{1,0:T(8,128)S(1)}, f32[32,128]{1,0:T(8,128)S(1)}, f32[1,128]{1,0:T(1,128)S(1)}, f32[8,128]{1,0:...) custom-call(f32[4096,1024]{1,0:T(8,128)} %bitcast.14, ...), custom_call_target="tpu_custom_call" | custom-call | tf_op jit(solution)/shard_map/pallas_call | solution.py:341
  163.5 3.4 %shard_map.144 = (f32[4096,128]{1,0:T(8,128)}, bf16[4096,128]{1,0:T(8,128)(2,1)}, f32[128,4096]{1,0:T(8,128)}, bf16[128,4096]{1,0:T(8,128)(2,1)}, f32[32,128]{1,...) custom-call(f32[4096,128]{1,0:T(8,128)S(1)} %get-tuple-element.26.refs_0_, ...), custom_call_target="tpu_custom_call" | custom-call | tf_op jit(solution)/shard_map/pallas_call | solution.py:397
Async XLA Ops:
  0.6 0.7 copy-start
  1.4 0.7 copy-start.1
  2.1 0.7 copy-start.2
  2.7 0.7 copy-start.3

commit v4 on v3

v4 whole, which is shorter than its diff:
```python
import functools

import jax
import jax.numpy as jnp
from jax import lax
from jax.experimental import pallas as pl
from jax.experimental.pallas import tpu as pltpu
from jax.sharding import PartitionSpec as P

TRAIN_STEP = 10
DECAY_EXP = 0.8
EPS_ONE = 1e-30
CLIP_LIMIT = 1.0
SCALE_FLOOR = 1e-3
LEARN_RATE = float(TRAIN_STEP) ** -0.5
BETA_TWO = 1.0 - float(TRAIN_STEP) ** -DECAY_EXP

MESH = pl.DeviceIdType.MESH
UNIT = 128
BIG = 2
EMB_SMALLS = 2
HEAD_SMALLS = 2
AHEAD = 4
LAGS = (2, 4, 5, 7, 9)
LANES = 128
VMEM_MIB = 45
PSTART = 4
RELAYED = LAGS[4] + 4


class Table:
    def __init__(self, is_emb, units, grad, param, outs, bufs, small, sems):
        self.is_emb, self.grad, self.param = is_emb, grad, param
        self.smalls = EMB_SMALLS if is_emb else HEAD_SMALLS
        self.bigs = (units - self.smalls) // BIG
        self.chunks = self.smalls + self.bigs
        self.dirn, self.pcopy, self.row_new, self.col_new, self.scale = outs
        self.own, self.half, self.first_x, self.first_y, self.second_x, self.second_y = bufs
        (self.rpart, self.rrecv, self.rsum, self.rall, self.col_acc, self.w_acc, self.r_acc, self.p_acc, self.colx, self.scalx,
         self.vec) = small
        (self.ld, self.ra, self.rfx, self.rfy, self.rgx, self.rgy, self.rr0, self.rr1, self.rr2, self.snd, self.one) = sems
        self.rr = (self.rr0, self.rr1, self.rr2)

    def span(self, k):
        if self.is_emb:
            small = k < self.smalls
            return jnp.where(small, k, self.smalls + (k - self.smalls) * BIG), small
        small = k >= self.bigs
        return jnp.where(small, self.bigs * BIG + k - self.bigs, k * BIG), small

    def sized(self, k, act):
        first, small = self.span(k)

        @pl.when(small)
        def _():
            act(first, 1)

        @pl.when(jnp.logical_not(small))
        def _():
            act(first, BIG)

    def units(self, k, act):
        first, small = self.span(k)

        def one(j, carry):
            act(first + j)
            return carry

        lax.fori_loop(0, jnp.where(small, 1, BIG), one, 0)


N_OUT, N_BUF, N_SMALL, N_SEM = 5, 6, 11, 11
HALF = UNIT // 2


def arrived(ref, sem):
    pltpu.make_async_copy(ref, ref, sem).wait()


def lane_sum(a):
    return jnp.sum(a, axis=1, keepdims=True)


def fold8(a):
    return jnp.sum(a.reshape(a.shape[0] // 8, 8, a.shape[1]), axis=0)


def adafactor_kernel(units, nz, nd, *refs):
    emb_in, head_in, old = refs[0:2], refs[2:4], refs[4]
    pos = 5
    emb_out, head_out = refs[pos:pos + N_OUT], refs[pos + N_OUT:pos + 2 * N_OUT]
    pos += 2 * N_OUT
    emb_buf, head_buf = refs[pos:pos + N_BUF], refs[pos + N_BUF:pos + 2 * N_BUF]
    pos += 2 * N_BUF
    emb_small, head_small = refs[pos:pos + N_SMALL], refs[pos + N_SMALL:pos + 2 * N_SMALL]
    pos += 2 * N_SMALL
    emb_sem, head_sem = refs[pos:pos + N_SEM], refs[pos + N_SEM:pos + 2 * N_SEM]
    token, rall_sem, rall_snd = refs[pos + 2 * N_SEM:]
    emb = Table(True, units, *emb_in, emb_out, emb_buf, emb_small, emb_sem)
    head = Table(False, units, *head_in, head_out, head_buf, head_small, head_sem)
    vocab, embed = float(nz * units * UNIT), float(nd * LANES)
    others = nz * nd - 1
    bigs = head.bigs
    chunks = emb.chunks
    total = emb.chunks + head.chunks

    z = lax.axis_index("model")
    d = lax.axis_index("data")
    me = z * nd + d
    c = lax.rem(d, 2)
    x = lax.rem(d // 2, 2)
    y = d // 4
    partner = (z, d + 1 - 2 * c)
    xnbr = (z, d + 2 - 4 * x)
    ynbr = (z, d + 4 - 8 * y)
    ring = (partner, xnbr, ynbr)

    def send(src, dst, ssem, rsem, to):
        pltpu.make_async_remote_copy(src_ref=src, dst_ref=dst, send_sem=ssem, recv_sem=rsem,
                                     device_id=to, device_id_type=MESH).start()

    def blocks(t, u, n, core, buf):
        if t.is_emb:
            for yy in range(2):
                for xx in range(2):
                    col = pl.multiple_of(((yy * 2 + xx) * 2 + core) * LANES, LANES)
                    yield t.grad.at[pl.ds(u, n), :, pl.ds(col, LANES)], buf.at[pl.ds(u, n), yy, xx]
        else:
            for j in range(n):
                lanes = pl.ds(pl.multiple_of((u + j) * UNIT, UNIT), UNIT)
                yield t.grad.at[:, :, core, :, lanes], buf.at[u + j]

    def load(k, t):
        def act(u, n):
            for src, dst in blocks(t, u, n, c, t.own):
                pltpu.make_async_copy(src, dst, t.ld.at[k]).start()
        t.sized(k, act)

    def exchange(k, t):
        def act(u, n):
            for src, dst in blocks(t, u, n, 1 - c, t.half):
                send(src, dst, t.snd.at[0], t.ra.at[k], partner)
        t.sized(k, act)

    def first_hop(k, t):
        def act(u, n):
            part = pl.ds(u, n)
            arrived(t.own.at[part], t.ld.at[k])
            arrived(t.half.at[part], t.ra.at[k])
            for j in range(n):
                for yy in range(2):
                    t.own[u + j, yy, 1 - x, :HALF] += t.half[u + j, yy, 1 - x, :HALF]
            send(t.own.at[part, :, 1 - x, pl.ds(0, HALF)], t.first_x.at[part], t.snd.at[1], t.rfx.at[k], xnbr)
            for j in range(n):
                for xx in range(2):
                    t.own[u + j, 1 - y, xx, HALF:] += t.half[u + j, 1 - y, xx, HALF:]
            send(t.own.at[part, 1 - y, :, pl.ds(HALF, HALF)], t.first_y.at[part], t.snd.at[2], t.rfy.at[k], ynbr)
        t.sized(k, act)

    def second_hop(k, t):
        def act(u, n):
            part = pl.ds(u, n)
            arrived(t.first_x.at[part], t.rfx.at[k])
            for j in range(n):
                t.own[u + j, 1 - y, x, :HALF] += t.half[u + j, 1 - y, x, :HALF] + t.first_x[u + j, 1 - y]
            send(t.own.at[part, 1 - y, x, pl.ds(0, HALF)], t.second_x.at[part], t.snd.at[3], t.rgx.at[k], ynbr)
            arrived(t.first_y.at[part], t.rfy.at[k])
            for j in range(n):
                t.own[u + j, y, 1 - x, HALF:] += t.half[u + j, y, 1 - x, HALF:] + t.first_y[u + j, 1 - x]
            send(t.own.at[part, y, 1 - x, pl.ds(HALF, HALF)], t.second_y.at[part], t.snd.at[4], t.rgy.at[k], xnbr)
        t.sized(k, act)

    def tile(u):
        return pl.ds(pl.multiple_of(u * UNIT, UNIT), UNIT)

    def finish(k, t):
        def landed(u, n):
            arrived(t.second_x.at[pl.ds(u, n)], t.rgx.at[k])
            arrived(t.second_y.at[pl.ds(u, n)], t.rgy.at[k])

        def one(u):
            first = t.own[u, y, x, :HALF] + t.half[u, y, x, :HALF] + t.first_x[u, y] + t.second_x[u]
            last = t.own[u, y, x, HALF:] + t.half[u, y, x, HALF:] + t.first_y[u, x] + t.second_y[u]
            sq_first = first * first + EPS_ONE
            sq_last = last * last + EPS_ONE
            if t.is_emb:
                t.dirn[pl.ds(pl.multiple_of(u * UNIT, HALF), HALF), :] = first
                t.dirn[pl.ds(pl.multiple_of(u * UNIT + HALF, HALF), HALF), :] = last
                t.col_acc[...] += fold8(sq_first) + fold8(sq_last)
                sq = jnp.transpose(jnp.concatenate([sq_first, sq_last], axis=0))
                t.rpart[0, u] = jnp.sum(fold8(sq), axis=0, keepdims=True)
            else:
                t.dirn[:HALF, tile(u)] = first
                t.dirn[HALF:, tile(u)] = last
                t.col_acc[:HALF] += sq_first
                t.col_acc[HALF:] += sq_last
                t.rpart[0, u] = jnp.sum(fold8(sq_first) + fold8(sq_last), axis=0, keepdims=True)

        def pass_on(u, n):
            if not t.is_emb and n == 1:
                def to_peer(o, carry):
                    send(t.rpart.at[0, u], t.rall.at[k - bigs, d], rall_snd.at[0], rall_sem.at[k - bigs],
                         (z, lax.rem(d + o, nd)))
                    return carry
                lax.fori_loop(1, nd, to_peer, 0)
            else:
                send(t.rpart.at[0, pl.ds(u, n)], t.rrecv.at[0, pl.ds(u, n)], t.snd.at[5], t.rr[0].at[k], ring[0])

        t.sized(k, landed)
        t.units(k, one)
        t.sized(k, pass_on)

    def row_hop(s, k, t):
        def act(u, n):
            if t.is_emb or n > 1:
                part = pl.ds(u, n)
                arrived(t.rrecv.at[s - 1, part], t.rr[s - 1].at[k])
                t.rpart[s, part] = t.rpart[s - 1, part] + t.rrecv[s - 1, part]
                send(t.rpart.at[s, part], t.rrecv.at[s, part], t.snd.at[5 + s], t.rr[s].at[k], ring[s])
        t.sized(k, act)

    def complete(k, t):
        def landed(u, n):
            if not t.is_emb and n == 1:
                arrived(t.rall.at[k - bigs, pl.ds(0, nd - 1)], rall_sem.at[k - bigs])
                t.rall[k - bigs, d] = t.rpart[0, u]
                total = t.rall[k - bigs, 0]
                for i in range(1, nd):
                    total = total + t.rall[k - bigs, i]
                t.rsum[u] = total
            else:
                part = pl.ds(u, n)
                arrived(t.rrecv.at[2, part], t.rr[2].at[k])
                t.rsum[part] = t.rpart[2, part] + t.rrecv[2, part]

        def one(u):
            row = u if t.is_emb else units + u
            new = BETA_TWO * old[pl.ds(row, 1), :] + (1.0 - BETA_TWO) * (t.rsum[u] / embed)
            t.row_new[pl.ds(u, 1), :] = new
            t.r_acc[...] += new
            line = jnp.broadcast_to(lax.rsqrt(new), (LANES, LANES))
            if t.is_emb:
                n = t.dirn[tile(u), :] * jnp.transpose(line)
                t.dirn[tile(u), :] = n
                t.w_acc[...] += fold8(n * n)
                p = t.pcopy[tile(u), :]
            else:
                n = t.dirn[:, tile(u)] * line
                t.dirn[:, tile(u)] = n
                t.w_acc[...] += n * n
                p = t.pcopy[:, tile(u)]
            t.p_acc[...] += fold8(p * p)

        t.sized(k, landed)
        t.units(k, one)

    def per_col(t, acc):
        a = acc[...]
        return jnp.sum(a if t.is_emb else jnp.transpose(a), axis=0, keepdims=True)

    def send_cols(t):
        t.vec[0] = per_col(t, t.col_acc)
        for o in range(1, nz):
            send(t.vec.at[0], t.colx.at[z], t.one.at[0], t.one.at[1], (lax.rem(z + o, nz), d))

    def send_scalars(t):
        arrived(t.colx.at[pl.ds(0, nz - 1)], t.one.at[1])
        t.colx[z] = t.vec[0]
        col_sq = t.colx[0]
        for i in range(1, nz):
            col_sq = col_sq + t.colx[i]
        at = 2 * units + (0 if t.is_emb else 1)
        new = BETA_TWO * old[at:at + 1, :] + (1.0 - BETA_TWO) * (col_sq / vocab)
        t.col_new[...] = new
        w = lane_sum(per_col(t, t.w_acc) / new)
        r = lane_sum(t.r_acc[...]) / nd
        p = lane_sum(jnp.sum(t.p_acc[...], axis=0, keepdims=True))
        lane = lax.broadcasted_iota(jnp.int32, (1, LANES), 1)
        t.vec[1] = jnp.where(lane == 0, w, jnp.where(lane == 1, r, jnp.where(lane == 2, p, 0.0)))

        def one(o, carry):
            to = lax.rem(me + o, others + 1)
            send(t.vec.at[1], t.scalx.at[me], t.one.at[2], t.one.at[3], (to // nd, lax.rem(to, nd)))
            return carry

        lax.fori_loop(1, others + 1, one, 0)

    def finish_scalars(t):
        arrived(t.scalx.at[pl.ds(0, others)], t.one.at[3])
        t.scalx[me] = t.vec[1]
        total = jnp.sum(t.scalx[...], axis=0)
        lane = lax.broadcasted_iota(jnp.int32, (1, LANES), 1)
        w, r, p = (lane_sum(jnp.where(lane == i, total, 0.0)) for i in range(3))
        row_mean = r / vocab
        update_rms = jnp.sqrt(w * row_mean / (vocab * embed))
        param_rms = jnp.sqrt(p / (vocab * embed))
        step_size = LEARN_RATE * jnp.maximum(SCALE_FLOOR, param_rms) / jnp.maximum(1.0, update_rms / CLIP_LIMIT)
        line = lax.rsqrt(t.col_new[...]) * (jnp.sqrt(row_mean) * step_size)
        if t.is_emb:
            t.scale[...] = jnp.broadcast_to(line, t.scale.shape)
        else:
            t.scale[...] = jnp.transpose(jnp.broadcast_to(line, (LANES, LANES)))

    barrier = pltpu.get_barrier_semaphore()
    above, below = (lax.rem(z + 1, nz), d), (lax.rem(z + nz - 1, nz), d)

    def greet(to):
        pl.semaphore_signal(barrier, inc=1, device_id=to, device_id_type=MESH)

    for peer in ring:
        greet(peer)

    @pl.when(z < nz - 1)
    def _():
        greet(above)

    @pl.when(z > 0)
    def _():
        greet(below)

    for k in range(AHEAD):
        load(k, emb)
    for t in (emb, head):
        for acc in (t.col_acc, t.w_acc, t.r_acc, t.p_acc):
            acc[...] = jnp.zeros_like(acc)
    pl.semaphore_wait(barrier, 3 + jnp.where(z < nz - 1, 1, 0) + jnp.where(z > 0, 1, 0))

    for k in range(AHEAD):
        exchange(k, emb)

    def both(k, act):
        @pl.when((k >= 0) & (k < chunks))
        def _():
            act(k, emb)

        @pl.when((k >= chunks) & (k < total))
        def _():
            act(k - chunks, head)

    def fetch(k, t):
        load(k, t)
        exchange(k, t)

    def relay(r):
        for turn, source, last, to, sem in ((z, 0, nz - 1, above, token.at[0]), (nz - 1 - z, nz - 1, 0, below, token.at[1])):
            @pl.when(r == turn)
            def _():
                @pl.when(z != source)
                def _():
                    pl.semaphore_wait(sem, 1)

                @pl.when(z != last)
                def _():
                    pl.semaphore_signal(sem, inc=1, device_id=to, device_id_type=MESH)

    def step(i, carry):
        both(i + AHEAD, fetch)
        both(i, first_hop)

        @pl.when(i == PSTART)
        def _():
            for t in (emb, head):
                pltpu.make_async_copy(t.param, t.pcopy, t.one.at[4]).start()

        both(i - LAGS[0], second_hop)

        @pl.when(i == LAGS[4] - 1)
        def _():
            for t in (emb, head):
                arrived(t.pcopy, t.one.at[4])

        both(i - LAGS[1], finish)
        relay(i - LAGS[4] - 1)

        @pl.when(i == chunks - 1 + RELAYED)
        def _():
            send_cols(emb)

        @pl.when(i == total - 1 + LAGS[1])
        def _():
            send_cols(head)

        both(i - LAGS[2], functools.partial(row_hop, 1))
        both(i - LAGS[3], functools.partial(row_hop, 2))
        both(i - LAGS[4], complete)

        @pl.when(i == chunks + RELAYED)
        def _():
            send_scalars(emb)

        @pl.when(i == chunks + RELAYED + 2)
        def _():
            finish_scalars(emb)

        return carry

    lax.fori_loop(0, total + LAGS[4], step, 0)
    send_scalars(head)
    finish_scalars(head)

    for t in (emb, head):
        arrived(t.half, t.snd.at[0])
        arrived(t.first_x, t.snd.at[1])
        arrived(t.first_y, t.snd.at[2])
        arrived(t.second_x, t.snd.at[3])
        arrived(t.second_y, t.snd.at[4])
        hopped = t.rpart if t.is_emb else t.rpart.at[:, pl.ds(0, bigs * BIG)]
        for s in range(3):
            arrived(hopped.at[s], t.snd.at[5 + s])
        arrived(t.colx.at[pl.ds(0, nz - 1)], t.one.at[0])
        arrived(t.scalx.at[pl.ds(0, others)], t.one.at[2])
    arrived(head.rall.at[:, pl.ds(0, nd - 1)], rall_snd.at[0])


def statistics(mesh, emb_grad, head_grad, emb_param, head_param, emb_row, emb_col, head_row, head_col):
    rows, embed = emb_grad.shape
    units = rows // UNIT
    nz, nd = mesh.shape["model"], mesh.shape["data"]
    f32 = jnp.float32
    old = jnp.concatenate([a.reshape(a.shape[0] // LANES, LANES) for a in (emb_row, head_row, emb_col, head_col)])

    buffers = [pltpu.VMEM((units, 2, 2, UNIT, LANES), f32), pltpu.VMEM((units, 2, 2, UNIT, LANES), f32),
               pltpu.VMEM((units, 2, HALF, LANES), f32), pltpu.VMEM((units, 2, HALF, LANES), f32),
               pltpu.VMEM((units, HALF, LANES), f32), pltpu.VMEM((units, HALF, LANES), f32)]

    def small(acc_rows):
        return [pltpu.VMEM((3, units, 1, LANES), f32), pltpu.VMEM((3, units, 1, LANES), f32),
                pltpu.VMEM((units, 1, LANES), f32), pltpu.VMEM((HEAD_SMALLS, nd, 1, LANES), f32),
                pltpu.VMEM((acc_rows, LANES), f32), pltpu.VMEM((acc_rows, LANES), f32),
                pltpu.VMEM((1, LANES), f32), pltpu.VMEM((8, LANES), f32),
                pltpu.VMEM((nz, 1, LANES), f32), pltpu.VMEM((nz * nd, 1, LANES), f32), pltpu.VMEM((2, 1, LANES), f32)]

    sems = [pltpu.SemaphoreType.DMA((units // BIG + 2,)) for _ in range(9)]
    sems += [pltpu.SemaphoreType.DMA((8,)), pltpu.SemaphoreType.DMA((5,))]

    def outs(shape, scale_rows):
        return [jax.ShapeDtypeStruct(shape, f32), jax.ShapeDtypeStruct(shape, f32),
                jax.ShapeDtypeStruct((units, LANES), f32), jax.ShapeDtypeStruct((1, LANES), f32),
                jax.ShapeDtypeStruct((scale_rows, LANES), f32)]

    hbm = pl.BlockSpec(memory_space=pltpu.HBM)
    vmem = pl.BlockSpec(memory_space=pltpu.VMEM)
    results = pl.pallas_call(
        functools.partial(adafactor_kernel, units, nz, nd),
        out_shape=outs((rows, LANES), 8) + outs((LANES, rows), LANES),
        in_specs=[hbm] * 4 + [vmem],
        out_specs=[vmem] * 10,
        scratch_shapes=(buffers + buffers + small(8) + small(LANES) + sems + sems
                        + [pltpu.SemaphoreType.REGULAR((2,)), pltpu.SemaphoreType.DMA((HEAD_SMALLS,)),
                           pltpu.SemaphoreType.DMA((1,))]),
        compiler_params=pltpu.CompilerParams(collective_id=0, has_side_effects=True, vmem_limit_bytes=VMEM_MIB * 2 ** 20),
    )(emb_grad.reshape(units, UNIT, embed), emb_param, head_grad.reshape(2, 2, 2, LANES, rows), head_param, old)
    return results[:5], results[5:]


PIECES = 8


def apply_kernel(rows, *refs):
    (emb_dir, emb_p, emb_r, emb_c, emb_s, head_dir, head_p, head_r, head_c, head_s,
     emb_new, emb_b16, head_new, head_b16, emb_ro, emb_co, head_ro, head_co,
     emb_tmp, emb_tmp16, head_tmp, head_tmp16, sem) = refs
    size = rows // PIECES

    def piece(j, carry):
        span = pl.ds(pl.multiple_of(j * size, size), size)
        new = emb_p[span, :] - emb_dir[span, :] * emb_s[0:1, :]
        emb_tmp[span, :] = new
        emb_tmp16[span, :] = new.astype(jnp.bfloat16)
        pltpu.make_async_copy(emb_tmp.at[span], emb_new.at[span], sem.at[0]).start()
        pltpu.make_async_copy(emb_tmp16.at[span], emb_b16.at[span], sem.at[1]).start()
        for i in range(size // LANES):
            cols = pl.ds(pl.multiple_of(j * size + i * LANES, LANES), LANES)
            new = head_p[:, cols] - head_dir[:, cols] * head_s[...]
            head_tmp[:, cols] = new
            head_tmp16[:, cols] = new.astype(jnp.bfloat16)
        pltpu.make_async_copy(head_tmp.at[:, span], head_new.at[:, span], sem.at[2]).start()
        pltpu.make_async_copy(head_tmp16.at[:, span], head_b16.at[:, span], sem.at[3]).start()
        return carry

    emb_ro[...] = emb_r[...]
    emb_co[...] = emb_c[...]
    head_ro[...] = head_r[...]
    head_co[...] = head_c[...]
    lax.fori_loop(0, PIECES, piece, 0)
    arrived(emb_new, sem.at[0])
    arrived(emb_b16, sem.at[1])
    arrived(head_new, sem.at[2])
    arrived(head_b16, sem.at[3])


def apply_update(emb, head):
    rows = emb[0].shape[0]
    f32, b16 = jnp.float32, jnp.bfloat16
    hbm = pl.BlockSpec(memory_space=pltpu.HBM)
    vmem = pl.BlockSpec(memory_space=pltpu.VMEM)
    shapes = ((rows, LANES), f32), ((rows, LANES), b16), ((LANES, rows), f32), ((LANES, rows), b16)
    small = ((rows // LANES, LANES), f32), ((1, LANES), f32)
    emb_new, emb_b16, head_new, head_b16, emb_r, emb_c, head_r, head_c = pl.pallas_call(
        functools.partial(apply_kernel, rows),
        out_shape=[jax.ShapeDtypeStruct(s, t) for s, t in shapes + small + small],
        in_specs=[vmem] * 10,
        out_specs=[hbm] * 4 + [vmem] * 4,
        scratch_shapes=[pltpu.VMEM(s, t) for s, t in shapes] + [pltpu.SemaphoreType.DMA((4,))],
        compiler_params=pltpu.CompilerParams(vmem_limit_bytes=24 * 2 ** 20),
    )(*emb, *head)
    return (emb_new, head_new, emb_r.reshape(rows), emb_c.reshape(LANES), head_r.reshape(rows), head_c.reshape(LANES),
            emb_b16, head_b16)


def solution(mesh):
    arg_specs = (P("model", "data"), P("data", "model"), P("data", "model", None), P("data", None, "model"),
                 P("model"), P("data"), P("model"), P("data"))
    result_specs = (P("model", "data"), P("data", "model"), P("model"), P("data"), P("model"), P("data"),
                    P("model", "data"), P("data", "model"))

    def local_step(emb_block, head_block, emb_contrib, head_contrib, emb_rows, emb_cols, head_rows, head_cols):
        emb, head = statistics(mesh, emb_contrib[0], head_contrib[0], emb_block, head_block,
                               emb_rows, emb_cols, head_rows, head_cols)
        return apply_update(emb, head)

    return jax.shard_map(local_step, mesh=mesh, in_specs=arg_specs, out_specs=result_specs, check_vma=False)
```

time: 167 us -> 163 us (0.976)
  Pallas kernels: 164 us -> 161 us
  local copies, waits for them, and re-layouts: 2.74 us -> 0 us
    unnamed x8 -> x0, local copies, waits for them, and re-layouts: 2.74 us -> none
    pallas_call x1, Pallas kernels: 160 us -> 158 us  [statistics(): pl.pallas_call(functools.partial(adafactor_kernel, units, nz, nd), out_sh...]
where the time goes in v4:
time: 163 us
  Pallas kernels  161 us (99%)
    pallas_call x1, Pallas kernels, statistics(): pl.pallas_call(functools.partial(adafactor_kernel, units, nz, nd), out_sh...  158 us
    pallas_call x1, Pallas kernels, apply_update(): pl.pallas_call(functools.partial(apply_kernel, rows), out_shape=[jax.Shap...  3.37 us

profile of v4, /device:TPU:0, one launch (start us, length us, event | category | flops | bytes accessed | tf_op | source)
XLA Modules:
  0.0 162.6 jit_solution(412110707801926186)
XLA Ops:
  0.6 0.8 pad_maximum_fusion.refs_4_
  1.4 157.8 %shard_map.143 = (f32[4096,128]{1,0:T(8,128)S(1)}, f32[4096,128]{1,0:T(8,128)S(1)}, f32[32,128]{1,0:T(8,128)S(1)}, f32[1,128]{1,0:T(1,128)S(1)}, f32[8,128]{1,0:...) custom-call(f32[32,128,1024]{2,1,0:T(8,128)} %bitcast.10, ...), custom_call_target="tpu_custom_call" | custom-call | tf_op jit(solution)/shard_map/pallas_call | solution.py:443
  159.2 3.4 %shard_map.144 = (f32[4096,128]{1,0:T(8,128)}, bf16[4096,128]{1,0:T(8,128)(2,1)}, f32[128,4096]{1,0:T(8,128)}, bf16[128,4096]{1,0:T(8,128)(2,1)}, f32[32,128]{1,...) custom-call(f32[4096,128]{1,0:T(8,128)S(1)} %get-tuple-element.26.refs_0_, ...), custom_call_target="tpu_custom_call" | custom-call | tf_op jit(solution)/shard_map/pallas_call | solution.py:499

commit v5 on v4

--- a/solution.py
+++ b/solution.py
@@ -17,9 +17,10 @@
 
 MESH = pl.DeviceIdType.MESH
 UNIT = 128
-BIG = 2
-EMB_SMALLS = 2
-HEAD_SMALLS = 2
+BIG = 4
+EMB_SMALLS = 4
+HEAD_SMALLS = 8
+DIRECT = 8
 AHEAD = 4
 LAGS = (2, 4, 5, 7, 9)
 LANES = 128
@@ -34,6 +35,7 @@
         self.smalls = EMB_SMALLS if is_emb else HEAD_SMALLS
         self.bigs = (units - self.smalls) // BIG
         self.chunks = self.smalls + self.bigs
+        self.hops = self.chunks if is_emb else self.chunks - DIRECT
         self.dirn, self.pcopy, self.row_new, self.col_new, self.scale = outs
         self.own, self.half, self.first_x, self.first_y, self.second_x, self.second_y = bufs
         (self.rpart, self.rrecv, self.rsum, self.rall, self.col_acc, self.w_acc, self.r_acc, self.p_acc, self.colx, self.scalx,
@@ -48,14 +50,14 @@
         small = k >= self.bigs
         return jnp.where(small, self.bigs * BIG + k - self.bigs, k * BIG), small
 
-    def sized(self, k, act):
+    def sized(self, k, act, when=True):
         first, small = self.span(k)
 
-        @pl.when(small)
+        @pl.when(small & when)
         def _():
             act(first, 1)
 
-        @pl.when(jnp.logical_not(small))
+        @pl.when(jnp.logical_not(small) & when)
         def _():
             act(first, BIG)
 
@@ -86,8 +88,8 @@
 
 
 def adafactor_kernel(units, nz, nd, *refs):
-    emb_in, head_in, old = refs[0:2], refs[2:4], refs[4]
-    pos = 5
+    emb_in, head_in, old_in = refs[0:2], refs[2:4], refs[4:8]
+    pos = 8
     emb_out, head_out = refs[pos:pos + N_OUT], refs[pos + N_OUT:pos + 2 * N_OUT]
     pos += 2 * N_OUT
     emb_buf, head_buf = refs[pos:pos + N_BUF], refs[pos + N_BUF:pos + 2 * N_BUF]
@@ -95,12 +97,13 @@
     emb_small, head_small = refs[pos:pos + N_SMALL], refs[pos + N_SMALL:pos + 2 * N_SMALL]
     pos += 2 * N_SMALL
     emb_sem, head_sem = refs[pos:pos + N_SEM], refs[pos + N_SEM:pos + 2 * N_SEM]
-    token, rall_sem, rall_snd = refs[pos + 2 * N_SEM:]
+    token, rall_sem, rall_snd, old, old_sem = refs[pos + 2 * N_SEM:]
     emb = Table(True, units, *emb_in, emb_out, emb_buf, emb_small, emb_sem)
     head = Table(False, units, *head_in, head_out, head_buf, head_small, head_sem)
     vocab, embed = float(nz * units * UNIT), float(nd * LANES)
     others = nz * nd - 1
-    bigs = head.bigs
+    old_rows = (0, units), (units, units), (2 * units, 1), (2 * units + 1, 1)
+    hop_units = head.hops * BIG
     chunks = emb.chunks
     total = emb.chunks + head.chunks
 
@@ -197,41 +200,40 @@
                 t.rpart[0, u] = jnp.sum(fold8(sq_first) + fold8(sq_last), axis=0, keepdims=True)
 
         def pass_on(u, n):
-            if not t.is_emb and n == 1:
-                def to_peer(o, carry):
-                    send(t.rpart.at[0, u], t.rall.at[k - bigs, d], rall_snd.at[0], rall_sem.at[k - bigs],
-                         (z, lax.rem(d + o, nd)))
-                    return carry
-                lax.fori_loop(1, nd, to_peer, 0)
-            else:
-                send(t.rpart.at[0, pl.ds(u, n)], t.rrecv.at[0, pl.ds(u, n)], t.snd.at[5], t.rr[0].at[k], ring[0])
+            send(t.rpart.at[0, pl.ds(u, n)], t.rrecv.at[0, pl.ds(u, n)], t.snd.at[5], t.rr[0].at[k], ring[0])
+
+        def to_all(u, n):
+            def to_peer(o, carry):
+                send(t.rpart.at[0, pl.ds(u, n)], t.rall.at[d, pl.ds(u - hop_units, n)], rall_snd.at[0],
+                     rall_sem.at[k - t.hops], (z, lax.rem(d + o, nd)))
+                return carry
+            lax.fori_loop(1, nd, to_peer, 0)
 
         t.sized(k, landed)
         t.units(k, one)
-        t.sized(k, pass_on)
+        t.sized(k, pass_on, k < t.hops)
+        if not t.is_emb:
+            t.sized(k, to_all, k >= t.hops)
 
     def row_hop(s, k, t):
         def act(u, n):
-            if t.is_emb or n > 1:
-                part = pl.ds(u, n)
-                arrived(t.rrecv.at[s - 1, part], t.rr[s - 1].at[k])
-                t.rpart[s, part] = t.rpart[s - 1, part] + t.rrecv[s - 1, part]
-                send(t.rpart.at[s, part], t.rrecv.at[s, part], t.snd.at[5 + s], t.rr[s].at[k], ring[s])
-        t.sized(k, act)
+            part = pl.ds(u, n)
+            arrived(t.rrecv.at[s - 1, part], t.rr[s - 1].at[k])
+            t.rpart[s, part] = t.rpart[s - 1, part] + t.rrecv[s - 1, part]
+            send(t.rpart.at[s, part], t.rrecv.at[s, part], t.snd.at[5 + s], t.rr[s].at[k], ring[s])
+        t.sized(k, act, k < t.hops)
 
     def complete(k, t):
         def landed(u, n):
-            if not t.is_emb and n == 1:
-                arrived(t.rall.at[k - bigs, pl.ds(0, nd - 1)], rall_sem.at[k - bigs])
-                t.rall[k - bigs, d] = t.rpart[0, u]
-                total = t.rall[k - bigs, 0]
-                for i in range(1, nd):
-                    total = total + t.rall[k - bigs, i]
-                t.rsum[u] = total
-            else:
-                part = pl.ds(u, n)
-                arrived(t.rrecv.at[2, part], t.rr[2].at[k])
-                t.rsum[part] = t.rpart[2, part] + t.rrecv[2, part]
+            part = pl.ds(u, n)
+            arrived(t.rrecv.at[2, part], t.rr[2].at[k])
+            t.rsum[part] = t.rpart[2, part] + t.rrecv[2, part]
+
+        def landed_all(u, n):
+            part = pl.ds(u - hop_units, n)
+            arrived(t.rall.at[pl.ds(0, nd - 1), part], rall_sem.at[k - t.hops])
+            t.rall[d, part] = t.rpart[0, pl.ds(u, n)]
+            t.rsum[pl.ds(u, n)] = jnp.sum(t.rall[:, part], axis=0)
 
         def one(u):
             row = u if t.is_emb else units + u
@@ -251,7 +253,9 @@
                 p = t.pcopy[:, tile(u)]
             t.p_acc[...] += fold8(p * p)
 
-        t.sized(k, landed)
+        t.sized(k, landed, k < t.hops)
+        if not t.is_emb:
+            t.sized(k, landed_all, k >= t.hops)
         t.units(k, one)
 
     def per_col(t, acc):
@@ -279,11 +283,16 @@
         t.vec[1] = jnp.where(lane == 0, w, jnp.where(lane == 1, r, jnp.where(lane == 2, p, 0.0)))
 
         def one(o, carry):
-            to = lax.rem(me + o, others + 1)
-            send(t.vec.at[1], t.scalx.at[me], t.one.at[2], t.one.at[3], (to // nd, lax.rem(to, nd)))
+            far = o // nd
+            plane = jnp.where(z < nz // 2, nz - 1 - far, far)
+            peer = lax.rem(d + o, nd)
+
+            @pl.when(plane * nd + peer != me)
+            def _():
+                send(t.vec.at[1], t.scalx.at[me], t.one.at[2], t.one.at[3], (plane, peer))
             return carry
 
-        lax.fori_loop(1, others + 1, one, 0)
+        lax.fori_loop(0, others + 1, one, 0)
 
     def finish_scalars(t):
         arrived(t.scalx.at[pl.ds(0, others)], t.one.at[3])
@@ -361,6 +370,8 @@
         def _():
             for t in (emb, head):
                 pltpu.make_async_copy(t.param, t.pcopy, t.one.at[4]).start()
+            for i, (first, n) in enumerate(old_rows):
+                pltpu.make_async_copy(old_in[i], old.at[pl.ds(first, n)], old_sem.at[i]).start()
 
         both(i - LAGS[0], second_hop)
 
@@ -368,6 +379,8 @@
         def _():
             for t in (emb, head):
                 arrived(t.pcopy, t.one.at[4])
+            for i, (first, n) in enumerate(old_rows):
+                arrived(old.at[pl.ds(first, n)], old_sem.at[i])
 
         both(i - LAGS[1], finish)
         relay(i - LAGS[4] - 1)
@@ -404,20 +417,22 @@
         arrived(t.first_y, t.snd.at[2])
         arrived(t.second_x, t.snd.at[3])
         arrived(t.second_y, t.snd.at[4])
-        hopped = t.rpart if t.is_emb else t.rpart.at[:, pl.ds(0, bigs * BIG)]
+        hopped = t.rpart if t.is_emb else t.rpart.at[:, pl.ds(0, hop_units)]
         for s in range(3):
             arrived(hopped.at[s], t.snd.at[5 + s])
         arrived(t.colx.at[pl.ds(0, nz - 1)], t.one.at[0])
         arrived(t.scalx.at[pl.ds(0, others)], t.one.at[2])
-    arrived(head.rall.at[:, pl.ds(0, nd - 1)], rall_snd.at[0])
+    arrived(head.rall.at[pl.ds(0, nd - 1)], rall_snd.at[0])
 
 
 def statistics(mesh, emb_grad, head_grad, emb_param, head_param, emb_row, emb_col, head_row, head_col):
     rows, embed = emb_grad.shape
     units = rows // UNIT
+    chunks = max(s + (units - s) // BIG for s in (EMB_SMALLS, HEAD_SMALLS))
     nz, nd = mesh.shape["model"], mesh.shape["data"]
     f32 = jnp.float32
-    old = jnp.concatenate([a.reshape(a.shape[0] // LANES, LANES) for a in (emb_row, head_row, emb_col, head_col)])
+    old = [pltpu.with_memory_space_constraint(a.reshape(a.shape[0] // LANES, LANES), pltpu.HBM)
+           for a in (emb_row, head_row, emb_col, head_col)]
 
     buffers = [pltpu.VMEM((units, 2, 2, UNIT, LANES), f32), pltpu.VMEM((units, 2, 2, UNIT, LANES), f32),
                pltpu.VMEM((units, 2, HALF, LANES), f32), pltpu.VMEM((units, 2, HALF, LANES), f32),
@@ -425,12 +440,12 @@
 
     def small(acc_rows):
         return [pltpu.VMEM((3, units, 1, LANES), f32), pltpu.VMEM((3, units, 1, LANES), f32),
-                pltpu.VMEM((units, 1, LANES), f32), pltpu.VMEM((HEAD_SMALLS, nd, 1, LANES), f32),
+                pltpu.VMEM((units, 1, LANES), f32), pltpu.VMEM((nd, HEAD_SMALLS + (DIRECT - HEAD_SMALLS) * BIG, 1, LANES), f32),
                 pltpu.VMEM((acc_rows, LANES), f32), pltpu.VMEM((acc_rows, LANES), f32),
                 pltpu.VMEM((1, LANES), f32), pltpu.VMEM((8, LANES), f32),
                 pltpu.VMEM((nz, 1, LANES), f32), pltpu.VMEM((nz * nd, 1, LANES), f32), pltpu.VMEM((2, 1, LANES), f32)]
 
-    sems = [pltpu.SemaphoreType.DMA((units // BIG + 2,)) for _ in range(9)]
+    sems = [pltpu.SemaphoreType.DMA((chunks,)) for _ in range(9)]
     sems += [pltpu.SemaphoreType.DMA((8,)), pltpu.SemaphoreType.DMA((5,))]
 
     def outs(shape, scale_rows):
@@ -443,13 +458,14 @@
     results = pl.pallas_call(
         functools.partial(adafactor_kernel, units, nz, nd),
         out_shape=outs((rows, LANES), 8) + outs((LANES, rows), LANES),
-        in_specs=[hbm] * 4 + [vmem],
+        in_specs=[hbm] * 8,
         out_specs=[vmem] * 10,
         scratch_shapes=(buffers + buffers + small(8) + small(LANES) + sems + sems
-                        + [pltpu.SemaphoreType.REGULAR((2,)), pltpu.SemaphoreType.DMA((HEAD_SMALLS,)),
-                           pltpu.SemaphoreType.DMA((1,))]),
+                        + [pltpu.SemaphoreType.REGULAR((2,)), pltpu.SemaphoreType.DMA((DIRECT,)),
+                           pltpu.SemaphoreType.DMA((1,)), pltpu.VMEM((2 * units + 2, LANES), f32),
+                           pltpu.SemaphoreType.DMA((4,))]),
         compiler_params=pltpu.CompilerParams(collective_id=0, has_side_effects=True, vmem_limit_bytes=VMEM_MIB * 2 ** 20),
-    )(emb_grad.reshape(units, UNIT, embed), emb_param, head_grad.reshape(2, 2, 2, LANES, rows), head_param, old)
+    )(emb_grad.reshape(units, UNIT, embed), emb_param, head_grad.reshape(2, 2, 2, LANES, rows), head_param, *old)
     return results[:5], results[5:]
 
 

time: 163 us -> 160 us (0.982)
  Pallas kernels: 161 us -> 159 us
    pallas_call x1, Pallas kernels: 158 us -> 156 us  [statistics(): pl.pallas_call(functools.partial(adafactor_kernel, units, nz, nd), out_sh...]
where the time goes in v5:
time: 160 us
  Pallas kernels  159 us (99%)
    pallas_call x1, Pallas kernels, statistics(): pl.pallas_call(functools.partial(adafactor_kernel, units, nz, nd), out_sh...  156 us
    pallas_call x1, Pallas kernels, apply_update(): pl.pallas_call(functools.partial(apply_kernel, rows), out_shape=[jax.Shap...  3.37 us

profile of v5, /device:TPU:0, one launch (start us, length us, event | category | flops | bytes accessed | tf_op | source)
XLA Modules:
  0.0 159.8 jit_solution(1372561651390655224)
XLA Ops:
  0.6 155.8 %shard_map.143 = (f32[4096,128]{1,0:T(8,128)S(1)}, f32[4096,128]{1,0:T(8,128)S(1)}, f32[32,128]{1,0:T(8,128)S(1)}, f32[1,128]{1,0:T(1,128)S(1)}, f32[8,128]{1,0:...) custom-call(f32[32,128,1024]{2,1,0:T(8,128)} %bitcast.10, ...), custom_call_target="tpu_custom_call" | custom-call | tf_op jit(solution)/shard_map/pallas_call | solution.py:458
  156.4 3.4 %shard_map.144 = (f32[4096,128]{1,0:T(8,128)}, bf16[4096,128]{1,0:T(8,128)(2,1)}, f32[128,4096]{1,0:T(8,128)}, bf16[128,4096]{1,0:T(8,128)(2,1)}, f32[32,128]{1,...) custom-call(f32[4096,128]{1,0:T(8,128)S(1)} %get-tuple-element.26.refs_0_, ...), custom_call_target="tpu_custom_call" | custom-call | tf_op jit(solution)/shard_map/pallas_call | solution.py:515

commit v6 on v5

--- a/solution.py
+++ b/solution.py
@@ -20,23 +20,27 @@
 BIG = 4
 EMB_SMALLS = 4
 HEAD_SMALLS = 8
-DIRECT = 8
+DIRECT = 4
 AHEAD = 4
 LAGS = (2, 4, 5, 7, 9)
 LANES = 128
-VMEM_MIB = 45
+VMEM_KIB = 47616
 PSTART = 4
-RELAYED = LAGS[4] + 4
 
 
 class Table:
-    def __init__(self, is_emb, units, grad, param, outs, bufs, small, sems):
+    def __init__(self, is_emb, units, grad, param, outs, bufs, small, sems, held=None):
         self.is_emb, self.grad, self.param = is_emb, grad, param
         self.smalls = EMB_SMALLS if is_emb else HEAD_SMALLS
         self.bigs = (units - self.smalls) // BIG
         self.chunks = self.smalls + self.bigs
         self.hops = self.chunks if is_emb else self.chunks - DIRECT
-        self.dirn, self.pcopy, self.row_new, self.col_new, self.scale = outs
+        self.hop_units = min(self.hops, self.bigs) * BIG + max(self.hops - self.bigs, 0)
+        if is_emb:
+            self.dirn, self.b16, self.row_new, self.col_new = outs
+            self.pcopy, self.scale = held
+        else:
+            self.dirn, self.pcopy, self.row_new, self.col_new, self.scale = outs
         self.own, self.half, self.first_x, self.first_y, self.second_x, self.second_y = bufs
         (self.rpart, self.rrecv, self.rsum, self.rall, self.col_acc, self.w_acc, self.r_acc, self.p_acc, self.colx, self.scalx,
          self.vec) = small
@@ -71,7 +75,7 @@
         lax.fori_loop(0, jnp.where(small, 1, BIG), one, 0)
 
 
-N_OUT, N_BUF, N_SMALL, N_SEM = 5, 6, 11, 11
+N_BUF, N_SMALL, N_SEM = 6, 11, 11
 HALF = UNIT // 2
 
 
@@ -90,20 +94,20 @@
 def adafactor_kernel(units, nz, nd, *refs):
     emb_in, head_in, old_in = refs[0:2], refs[2:4], refs[4:8]
     pos = 8
-    emb_out, head_out = refs[pos:pos + N_OUT], refs[pos + N_OUT:pos + 2 * N_OUT]
-    pos += 2 * N_OUT
+    emb_out, head_out = refs[pos:pos + 4], refs[pos + 4:pos + 9]
+    pos += 9
     emb_buf, head_buf = refs[pos:pos + N_BUF], refs[pos + N_BUF:pos + 2 * N_BUF]
     pos += 2 * N_BUF
     emb_small, head_small = refs[pos:pos + N_SMALL], refs[pos + N_SMALL:pos + 2 * N_SMALL]
     pos += 2 * N_SMALL
     emb_sem, head_sem = refs[pos:pos + N_SEM], refs[pos + N_SEM:pos + 2 * N_SEM]
-    token, rall_sem, rall_snd, old, old_sem = refs[pos + 2 * N_SEM:]
-    emb = Table(True, units, *emb_in, emb_out, emb_buf, emb_small, emb_sem)
+    token, rall_sem, rall_snd, old, old_sem, *held = refs[pos + 2 * N_SEM:]
+    emb = Table(True, units, *emb_in, emb_out, emb_buf, emb_small, emb_sem, held)
     head = Table(False, units, *head_in, head_out, head_buf, head_small, head_sem)
     vocab, embed = float(nz * units * UNIT), float(nd * LANES)
     others = nz * nd - 1
     old_rows = (0, units), (units, units), (2 * units, 1), (2 * units + 1, 1)
-    hop_units = head.hops * BIG
+    hop_units = head.hop_units
     chunks = emb.chunks
     total = emb.chunks + head.chunks
 
@@ -203,16 +207,18 @@
             send(t.rpart.at[0, pl.ds(u, n)], t.rrecv.at[0, pl.ds(u, n)], t.snd.at[5], t.rr[0].at[k], ring[0])
 
         def to_all(u, n):
-            def to_peer(o, carry):
+            for o in range(1, nd):
                 send(t.rpart.at[0, pl.ds(u, n)], t.rall.at[d, pl.ds(u - hop_units, n)], rall_snd.at[0],
                      rall_sem.at[k - t.hops], (z, lax.rem(d + o, nd)))
-                return carry
-            lax.fori_loop(1, nd, to_peer, 0)
 
         t.sized(k, landed)
         t.units(k, one)
         t.sized(k, pass_on, k < t.hops)
         if not t.is_emb:
+            @pl.when(k == t.chunks - 1)
+            def _():
+                send_cols(t)
+
             t.sized(k, to_all, k >= t.hops)
 
     def row_hop(s, k, t):
@@ -268,33 +274,36 @@
             send(t.vec.at[0], t.colx.at[z], t.one.at[0], t.one.at[1], (lax.rem(z + o, nz), d))
 
     def send_scalars(t):
+        per_col_w = per_col(t, t.w_acc)
+        r = lane_sum(t.r_acc[...]) / nd
+        p = lane_sum(jnp.sum(t.p_acc[...], axis=0, keepdims=True))
+        lane = lax.broadcasted_iota(jnp.int32, (1, LANES), 1)
+        rest = jnp.where(lane == 1, r, jnp.where(lane == 2, p, 0.0))
+        at = 2 * units + (0 if t.is_emb else 1)
+        kept = BETA_TWO * old[at:at + 1, :]
         arrived(t.colx.at[pl.ds(0, nz - 1)], t.one.at[1])
         t.colx[z] = t.vec[0]
         col_sq = t.colx[0]
         for i in range(1, nz):
             col_sq = col_sq + t.colx[i]
-        at = 2 * units + (0 if t.is_emb else 1)
-        new = BETA_TWO * old[at:at + 1, :] + (1.0 - BETA_TWO) * (col_sq / vocab)
+        new = kept + (1.0 - BETA_TWO) * (col_sq / vocab)
         t.col_new[...] = new
-        w = lane_sum(per_col(t, t.w_acc) / new)
-        r = lane_sum(t.r_acc[...]) / nd
-        p = lane_sum(jnp.sum(t.p_acc[...], axis=0, keepdims=True))
-        lane = lax.broadcasted_iota(jnp.int32, (1, LANES), 1)
-        t.vec[1] = jnp.where(lane == 0, w, jnp.where(lane == 1, r, jnp.where(lane == 2, p, 0.0)))
-
-        def one(o, carry):
-            far = o // nd
+        t.vec[1] = jnp.where(lane == 0, lane_sum(per_col_w / new), rest)
+        for far in range(nz):
             plane = jnp.where(z < nz // 2, nz - 1 - far, far)
-            peer = lax.rem(d + o, nd)
-
-            @pl.when(plane * nd + peer != me)
+            for o in range(1, nd):
+                send(t.vec.at[1], t.scalx.at[me], t.one.at[2], t.one.at[3], (plane, lax.rem(d + o, nd)))
+
+            @pl.when(plane != z)
             def _():
-                send(t.vec.at[1], t.scalx.at[me], t.one.at[2], t.one.at[3], (plane, peer))
-            return carry
-
-        lax.fori_loop(0, others + 1, one, 0)
+                send(t.vec.at[1], t.scalx.at[me], t.one.at[2], t.one.at[3], (plane, d))
 
     def finish_scalars(t):
+        line = lax.rsqrt(t.col_new[...])
+        if t.is_emb:
+            t.scale[...] = line
+        else:
+            t.scale[...] = jnp.transpose(jnp.broadcast_to(line, (LANES, LANES)))
         arrived(t.scalx.at[pl.ds(0, others)], t.one.at[3])
         t.scalx[me] = t.vec[1]
         total = jnp.sum(t.scalx[...], axis=0)
@@ -304,11 +313,16 @@
         update_rms = jnp.sqrt(w * row_mean / (vocab * embed))
         param_rms = jnp.sqrt(p / (vocab * embed))
         step_size = LEARN_RATE * jnp.maximum(SCALE_FLOOR, param_rms) / jnp.maximum(1.0, update_rms / CLIP_LIMIT)
-        line = lax.rsqrt(t.col_new[...]) * (jnp.sqrt(row_mean) * step_size)
-        if t.is_emb:
-            t.scale[...] = jnp.broadcast_to(line, t.scale.shape)
-        else:
-            t.scale[...] = jnp.transpose(jnp.broadcast_to(line, (LANES, LANES)))
+        t.scale[...] = t.scale[...] * (jnp.sqrt(row_mean) * step_size)
+
+    def update_emb():
+        def one(u, carry):
+            new = emb.pcopy[tile(u), :] - emb.dirn[tile(u), :] * emb.scale[...]
+            emb.dirn[tile(u), :] = new
+            emb.b16[tile(u), :] = new.astype(jnp.bfloat16)
+            return carry
+
+        lax.fori_loop(0, units, one, 0)
 
     barrier = pltpu.get_barrier_semaphore()
     above, below = (lax.rem(z + 1, nz), d), (lax.rem(z + nz - 1, nz), d)
@@ -362,6 +376,8 @@
                 def _():
                     pl.semaphore_signal(sem, inc=1, device_id=to, device_id_type=MESH)
 
+    known = max(chunks - 1 + LAGS[1], LAGS[4] + 1 + nz)
+
     def step(i, carry):
         both(i + AHEAD, fetch)
         both(i, first_hop)
@@ -385,30 +401,24 @@
         both(i - LAGS[1], finish)
         relay(i - LAGS[4] - 1)
 
-        @pl.when(i == chunks - 1 + RELAYED)
+        @pl.when(i == known)
         def _():
             send_cols(emb)
-
-        @pl.when(i == total - 1 + LAGS[1])
-        def _():
-            send_cols(head)
 
         both(i - LAGS[2], functools.partial(row_hop, 1))
         both(i - LAGS[3], functools.partial(row_hop, 2))
         both(i - LAGS[4], complete)
 
-        @pl.when(i == chunks + RELAYED)
+        @pl.when(i == total + 2)
         def _():
             send_scalars(emb)
-
-        @pl.when(i == chunks + RELAYED + 2)
-        def _():
-            finish_scalars(emb)
 
         return carry
 
     lax.fori_loop(0, total + LAGS[4], step, 0)
     send_scalars(head)
+    finish_scalars(emb)
+    update_emb()
     finish_scalars(head)
 
     for t in (emb, head):
@@ -440,7 +450,7 @@
 
     def small(acc_rows):
         return [pltpu.VMEM((3, units, 1, LANES), f32), pltpu.VMEM((3, units, 1, LANES), f32),
-                pltpu.VMEM((units, 1, LANES), f32), pltpu.VMEM((nd, HEAD_SMALLS + (DIRECT - HEAD_SMALLS) * BIG, 1, LANES), f32),
+                pltpu.VMEM((units, 1, LANES), f32), pltpu.VMEM((nd, min(DIRECT, HEAD_SMALLS) + max(DIRECT - HEAD_SMALLS, 0) * BIG, 1, LANES), f32),
                 pltpu.VMEM((acc_rows, LANES), f32), pltpu.VMEM((acc_rows, LANES), f32),
                 pltpu.VMEM((1, LANES), f32), pltpu.VMEM((8, LANES), f32),
                 pltpu.VMEM((nz, 1, LANES), f32), pltpu.VMEM((nz * nd, 1, LANES), f32), pltpu.VMEM((2, 1, LANES), f32)]
@@ -448,78 +458,69 @@
     sems = [pltpu.SemaphoreType.DMA((chunks,)) for _ in range(9)]
     sems += [pltpu.SemaphoreType.DMA((8,)), pltpu.SemaphoreType.DMA((5,))]
 
-    def outs(shape, scale_rows):
-        return [jax.ShapeDtypeStruct(shape, f32), jax.ShapeDtypeStruct(shape, f32),
-                jax.ShapeDtypeStruct((units, LANES), f32), jax.ShapeDtypeStruct((1, LANES), f32),
-                jax.ShapeDtypeStruct((scale_rows, LANES), f32)]
-
+    stats = [jax.ShapeDtypeStruct((units, LANES), f32), jax.ShapeDtypeStruct((1, LANES), f32)]
+    emb_outs = [jax.ShapeDtypeStruct((rows, LANES), f32), jax.ShapeDtypeStruct((rows, LANES), jnp.bfloat16)] + stats
+    head_outs = [jax.ShapeDtypeStruct((LANES, rows), f32)] * 2 + stats + [jax.ShapeDtypeStruct((LANES, LANES), f32)]
     hbm = pl.BlockSpec(memory_space=pltpu.HBM)
     vmem = pl.BlockSpec(memory_space=pltpu.VMEM)
     results = pl.pallas_call(
         functools.partial(adafactor_kernel, units, nz, nd),
-        out_shape=outs((rows, LANES), 8) + outs((LANES, rows), LANES),
+        out_shape=emb_outs + head_outs,
         in_specs=[hbm] * 8,
-        out_specs=[vmem] * 10,
+        out_specs=[vmem] * 9,
         scratch_shapes=(buffers + buffers + small(8) + small(LANES) + sems + sems
                         + [pltpu.SemaphoreType.REGULAR((2,)), pltpu.SemaphoreType.DMA((DIRECT,)),
                            pltpu.SemaphoreType.DMA((1,)), pltpu.VMEM((2 * units + 2, LANES), f32),
-                           pltpu.SemaphoreType.DMA((4,))]),
-        compiler_params=pltpu.CompilerParams(collective_id=0, has_side_effects=True, vmem_limit_bytes=VMEM_MIB * 2 ** 20),
+                           pltpu.SemaphoreType.DMA((4,)), pltpu.VMEM((rows, LANES), f32), pltpu.VMEM((1, LANES), f32)]),
+        compiler_params=pltpu.CompilerParams(collective_id=0, has_side_effects=True, vmem_limit_bytes=VMEM_KIB * 1024),
     )(emb_grad.reshape(units, UNIT, embed), emb_param, head_grad.reshape(2, 2, 2, LANES, rows), head_param, *old)
-    return results[:5], results[5:]
+    return results
 
 
 PIECES = 8
 
 
 def apply_kernel(rows, *refs):
-    (emb_dir, emb_p, emb_r, emb_c, emb_s, head_dir, head_p, head_r, head_c, head_s,
-     emb_new, emb_b16, head_new, head_b16, emb_ro, emb_co, head_ro, head_co,
-     emb_tmp, emb_tmp16, head_tmp, head_tmp16, sem) = refs
+    ready, (head_dir, head_p, head_r, head_c, head_s) = refs[:4], refs[4:9]
+    out, (head_new, head_b16, head_ro, head_co) = refs[9:13], refs[13:17]
+    head_tmp, head_tmp16, sem = refs[17:]
+    for i, (src, dst) in enumerate(zip(ready + (head_r, head_c), out + (head_ro, head_co))):
+        pltpu.make_async_copy(src, dst, sem.at[2 + i]).start()
     size = rows // PIECES
 
     def piece(j, carry):
         span = pl.ds(pl.multiple_of(j * size, size), size)
-        new = emb_p[span, :] - emb_dir[span, :] * emb_s[0:1, :]
-        emb_tmp[span, :] = new
-        emb_tmp16[span, :] = new.astype(jnp.bfloat16)
-        pltpu.make_async_copy(emb_tmp.at[span], emb_new.at[span], sem.at[0]).start()
-        pltpu.make_async_copy(emb_tmp16.at[span], emb_b16.at[span], sem.at[1]).start()
         for i in range(size // LANES):
             cols = pl.ds(pl.multiple_of(j * size + i * LANES, LANES), LANES)
             new = head_p[:, cols] - head_dir[:, cols] * head_s[...]
             head_tmp[:, cols] = new
             head_tmp16[:, cols] = new.astype(jnp.bfloat16)
-        pltpu.make_async_copy(head_tmp.at[:, span], head_new.at[:, span], sem.at[2]).start()
-        pltpu.make_async_copy(head_tmp16.at[:, span], head_b16.at[:, span], sem.at[3]).start()
+        pltpu.make_async_copy(head_tmp.at[:, span], head_new.at[:, span], sem.at[0]).start()
+        pltpu.make_async_copy(head_tmp16.at[:, span], head_b16.at[:, span], sem.at[1]).start()
         return carry
 
-    emb_ro[...] = emb_r[...]
-    emb_co[...] = emb_c[...]
-    head_ro[...] = head_r[...]
-    head_co[...] = head_c[...]
     lax.fori_loop(0, PIECES, piece, 0)
-    arrived(emb_new, sem.at[0])
-    arrived(emb_b16, sem.at[1])
-    arrived(head_new, sem.at[2])
-    arrived(head_b16, sem.at[3])
-
-
-def apply_update(emb, head):
-    rows = emb[0].shape[0]
+    arrived(head_new, sem.at[0])
+    arrived(head_b16, sem.at[1])
+    for i, dst in enumerate(out + (head_ro, head_co)):
+        arrived(dst, sem.at[2 + i])
+
+
+def apply_update(results):
+    rows = results[0].shape[0]
     f32, b16 = jnp.float32, jnp.bfloat16
     hbm = pl.BlockSpec(memory_space=pltpu.HBM)
     vmem = pl.BlockSpec(memory_space=pltpu.VMEM)
-    shapes = ((rows, LANES), f32), ((rows, LANES), b16), ((LANES, rows), f32), ((LANES, rows), b16)
-    small = ((rows // LANES, LANES), f32), ((1, LANES), f32)
-    emb_new, emb_b16, head_new, head_b16, emb_r, emb_c, head_r, head_c = pl.pallas_call(
+    stats = ((rows // LANES, LANES), f32), ((1, LANES), f32)
+    shapes = (((rows, LANES), f32), ((rows, LANES), b16)) + stats + (((LANES, rows), f32), ((LANES, rows), b16)) + stats
+    emb_new, emb_b16, emb_r, emb_c, head_new, head_b16, head_r, head_c = pl.pallas_call(
         functools.partial(apply_kernel, rows),
-        out_shape=[jax.ShapeDtypeStruct(s, t) for s, t in shapes + small + small],
-        in_specs=[vmem] * 10,
-        out_specs=[hbm] * 4 + [vmem] * 4,
-        scratch_shapes=[pltpu.VMEM(s, t) for s, t in shapes] + [pltpu.SemaphoreType.DMA((4,))],
+        out_shape=[jax.ShapeDtypeStruct(s, t) for s, t in shapes],
+        in_specs=[vmem] * 9,
+        out_specs=[hbm] * 8,
+        scratch_shapes=[pltpu.VMEM((LANES, rows), f32), pltpu.VMEM((LANES, rows), b16), pltpu.SemaphoreType.DMA((8,))],
         compiler_params=pltpu.CompilerParams(vmem_limit_bytes=24 * 2 ** 20),
-    )(*emb, *head)
+    )(*results)
     return (emb_new, head_new, emb_r.reshape(rows), emb_c.reshape(LANES), head_r.reshape(rows), head_c.reshape(LANES),
             emb_b16, head_b16)
 
@@ -531,8 +532,7 @@
                     P("model", "data"), P("data", "model"))
 
     def local_step(emb_block, head_block, emb_contrib, head_contrib, emb_rows, emb_cols, head_rows, head_cols):
-        emb, head = statistics(mesh, emb_contrib[0], head_contrib[0], emb_block, head_block,
-                               emb_rows, emb_cols, head_rows, head_cols)
-        return apply_update(emb, head)
+        return apply_update(statistics(mesh, emb_contrib[0], head_contrib[0], emb_block, head_block,
+                                       emb_rows, emb_cols, head_rows, head_cols))
 
     return jax.shard_map(local_step, mesh=mesh, in_specs=arg_specs, out_specs=result_specs, check_vma=False)

time: 160 us -> 159 us (level)
  no operation moved by 1% of the time
where the time goes in v6:
time: 159 us
  Pallas kernels  158 us (99%)
    pallas_call x1, Pallas kernels, statistics(): pl.pallas_call(functools.partial(adafactor_kernel, units, nz, nd), out_sh...  155 us

profile of v6, /device:TPU:0, one launch (start us, length us, event | category | flops | bytes accessed | tf_op | source)
XLA Modules:
  0.0 158.6 jit_solution(15903010774728069908)
XLA Ops:
  0.6 155.3 %shard_map.143 = (f32[4096,128]{1,0:T(8,128)S(1)}, bf16[4096,128]{1,0:T(8,128)(2,1)S(1)}, f32[32,128]{1,0:T(8,128)S(1)}, f32[1,128]{1,0:T(1,128)S(1)}, f32[128,4...) custom-call(f32[32,128,1024]{2,1,0:T(8,128)} %bitcast.10, ...), custom_call_target="tpu_custom_call" | custom-call | tf_op jit(solution)/shard_map/pallas_call | solution.py:466
  155.9 2.7 %shard_map.144 = (f32[4096,128]{1,0:T(8,128)}, bf16[4096,128]{1,0:T(8,128)(2,1)}, f32[32,128]{1,0:T(8,128)}, f32[1,128]{1,0:T(1,128)}, f32[128,4096]{1,0:T(8,128...) custom-call(f32[4096,128]{1,0:T(8,128)S(1)} %get-tuple-element.25.refs_0_, ...), custom_call_target="tpu_custom_call" | custom-call | tf_op jit(solution)/shard_map/pallas_call | solution.py:516

commit v7 on v6

--- a/solution.py
+++ b/solution.py
@@ -19,7 +19,7 @@
 UNIT = 128
 BIG = 4
 EMB_SMALLS = 4
-HEAD_SMALLS = 8
+HEAD_SMALLS = 4
 DIRECT = 4
 AHEAD = 4
 LAGS = (2, 4, 5, 7, 9)
@@ -273,12 +273,7 @@
         for o in range(1, nz):
             send(t.vec.at[0], t.colx.at[z], t.one.at[0], t.one.at[1], (lax.rem(z + o, nz), d))
 
-    def send_scalars(t):
-        per_col_w = per_col(t, t.w_acc)
-        r = lane_sum(t.r_acc[...]) / nd
-        p = lane_sum(jnp.sum(t.p_acc[...], axis=0, keepdims=True))
-        lane = lax.broadcasted_iota(jnp.int32, (1, LANES), 1)
-        rest = jnp.where(lane == 1, r, jnp.where(lane == 2, p, 0.0))
+    def columns(t):
         at = 2 * units + (0 if t.is_emb else 1)
         kept = BETA_TWO * old[at:at + 1, :]
         arrived(t.colx.at[pl.ds(0, nz - 1)], t.one.at[1])
@@ -288,7 +283,15 @@
             col_sq = col_sq + t.colx[i]
         new = kept + (1.0 - BETA_TWO) * (col_sq / vocab)
         t.col_new[...] = new
-        t.vec[1] = jnp.where(lane == 0, lane_sum(per_col_w / new), rest)
+        inverse = 1.0 / new
+        t.scale[...] = inverse if t.is_emb else jnp.transpose(jnp.broadcast_to(inverse, (LANES, LANES)))
+
+    def send_scalars(t):
+        w = lane_sum(jnp.sum(fold8(t.w_acc[...] * t.scale[...]), axis=0, keepdims=True))
+        r = lane_sum(t.r_acc[...]) / nd
+        p = lane_sum(jnp.sum(t.p_acc[...], axis=0, keepdims=True))
+        lane = lax.broadcasted_iota(jnp.int32, (1, LANES), 1)
+        t.vec[1] = jnp.where(lane == 0, w, jnp.where(lane == 1, r, jnp.where(lane == 2, p, 0.0)))
         for far in range(nz):
             plane = jnp.where(z < nz // 2, nz - 1 - far, far)
             for o in range(1, nd):
@@ -407,10 +410,16 @@
 
         both(i - LAGS[2], functools.partial(row_hop, 1))
         both(i - LAGS[3], functools.partial(row_hop, 2))
+
+        @pl.when(i == total - 1 + LAGS[4])
+        def _():
+            columns(head)
+
         both(i - LAGS[4], complete)
 
         @pl.when(i == total + 2)
         def _():
+            columns(emb)
             send_scalars(emb)
 
         return carry

time: 159 us -> 158 us (level)
  no operation moved by 1% of the time
where the time goes in v7:
time: 158 us
  Pallas kernels  157 us (99%)
    pallas_call x1, Pallas kernels, statistics(): pl.pallas_call(functools.partial(adafactor_kernel, units, nz, nd), out_sh...  155 us

profile of v7, /device:TPU:0, one launch (start us, length us, event | category | flops | bytes accessed | tf_op | source)
XLA Modules:
  0.0 158.0 jit_solution(1888304209855514586)
XLA Ops:
  0.6 154.6 %shard_map.143 = (f32[4096,128]{1,0:T(8,128)S(1)}, bf16[4096,128]{1,0:T(8,128)(2,1)S(1)}, f32[32,128]{1,0:T(8,128)S(1)}, f32[1,128]{1,0:T(1,128)S(1)}, f32[128,4...) custom-call(f32[32,128,1024]{2,1,0:T(8,128)} %bitcast.10, ...), custom_call_target="tpu_custom_call" | custom-call | tf_op jit(solution)/shard_map/pallas_call | solution.py:475
  155.2 2.7 %shard_map.144 = (f32[4096,128]{1,0:T(8,128)}, bf16[4096,128]{1,0:T(8,128)(2,1)}, f32[32,128]{1,0:T(8,128)}, f32[1,128]{1,0:T(1,128)}, f32[128,4096]{1,0:T(8,128...) custom-call(f32[4096,128]{1,0:T(8,128)S(1)} %get-tuple-element.25.refs_0_, ...), custom_call_target="tpu_custom_call" | custom-call | tf_op jit(solution)/shard_map/pallas_call | solution.py:525

commit v8 on v7

--- a/solution.py
+++ b/solution.py
@@ -17,7 +17,7 @@
 
 MESH = pl.DeviceIdType.MESH
 UNIT = 128
-BIG = 4
+BIG = 7
 EMB_SMALLS = 4
 HEAD_SMALLS = 4
 DIRECT = 4

time: 158 us -> 158 us (level)
  no operation moved by 1% of the time
where the time goes in v8:
time: 158 us; the launch traced here: 157 us
  Pallas kernels  157 us (99%)
    pallas_call x1, Pallas kernels, statistics(): pl.pallas_call(functools.partial(adafactor_kernel, units, nz, nd), out_sh...  154 us

profile of v8, /device:TPU:0, one launch (start us, length us, event | category | flops | bytes accessed | tf_op | source)
XLA Modules:
  0.0 157.4 jit_solution(10703104025456112413)
XLA Ops:
  0.6 154.0 %shard_map.143 = (f32[4096,128]{1,0:T(8,128)S(1)}, bf16[4096,128]{1,0:T(8,128)(2,1)S(1)}, f32[32,128]{1,0:T(8,128)S(1)}, f32[1,128]{1,0:T(1,128)S(1)}, f32[128,4...) custom-call(f32[32,128,1024]{2,1,0:T(8,128)} %bitcast.10, ...), custom_call_target="tpu_custom_call" | custom-call | tf_op jit(solution)/shard_map/pallas_call | solution.py:475
  154.7 2.7 %shard_map.144 = (f32[4096,128]{1,0:T(8,128)}, bf16[4096,128]{1,0:T(8,128)(2,1)}, f32[32,128]{1,0:T(8,128)}, f32[1,128]{1,0:T(1,128)}, f32[128,4096]{1,0:T(8,128...) custom-call(f32[4096,128]{1,0:T(8,128)S(1)} %get-tuple-element.25.refs_0_, ...), custom_call_target="tpu_custom_call" | custom-call | tf_op jit(solution)/shard_map/pallas_call | solution.py:525
